TPU v7x, 256 devices: a whole 4x4x8 slice. The times are simulated.
256 devices in a mesh: dp: 128 (over z, x, y_hi, core), tensor: 2 (over y_lo).
Axes of the slice: x: 4, y: 4 (y_hi: 2, y_lo: 2; y = y_hi * 2 + y_lo), z: 8, core: 2. Of those that a mesh axis runs over, the one named last changes fastest.
Arguments:
- tokens: bfloat16 [16384, 2048], P('dp'), may hold values from -16 to 16
- teacher: bfloat16 [16384, 2048], P('dp'), may hold values from -6 to 6
- inner_weight: float32 [2048, 512], P('dp', 'tensor'), may hold values from -0.125 to 0.125
- output_weight: bfloat16 [2048, 2048], P('dp', 'tensor'), may hold values from -0.125 to 0.125
- inner_first: float32 [2048, 512], P('dp', 'tensor'), may hold values from -2 to 2
- inner_second: float32 [2048, 512], P('dp', 'tensor'), may hold values from 0.2 to 2
- state_weight: bfloat16 [2048, 32], replicated, may hold values from -0.03125 to 0.03125
- step_weight: bfloat16 [2048, 16], P(None, 'tensor'), may hold values from -0.0390625 to 0.0390625
- step_bias: float32 [16], P('tensor'), may hold values from -4 to 0
- decay_log: float32 [16], P('tensor'), may hold values from -3 to 1
- skip_gain: float32 [16], P('tensor'), may hold values from 0.5 to 1.5
Outputs:
- distill_loss: float32 [], replicated
- inner_update: float32 [2048, 512], P('dp', 'tensor')
- inner_first_next: float32 [2048, 512], P('dp', 'tensor')
- inner_second_next: float32 [2048, 512], P('dp', 'tensor')
All inputs are finite; a program needn't handle non-finite values.
Results may differ from a plain program's by a relative error of at most 0.0016.
Values may be sent and summed in bfloat16 or wider, within the bound.
A program may use at most 64 MiB of HBM per device.

v0:
```python
import jax
import jax.numpy as jnp
from jax import lax
from jax.sharding import Mesh
from jax.sharding import PartitionSpec as P

HEADS = 16
GROUPS = 4
HEAD_DIM = 128
STEP = 20
DP = ("dp_0", "dp_1", "dp_2", "dp_3")
DP_TENSOR = ("dp_0", "dp_1", "dp_2", "dp_3", "tensor")


beta_one = 0.9
beta_two = 0.95
adam_eps = 1e-08
weight_decay = 0.1
norm_eps = 1e-06


def sent_together(arrays, axis, dim, along):
    widths = [a.shape[along] for a in arrays]
    both = jnp.concatenate(arrays, axis=along)
    whole = lax.all_gather(both, axis, axis=dim, tiled=True)
    return tuple(jnp.split(whole, [sum(widths[:k]) for k in range(1, len(widths))], axis=along))


def sent_to_all(x, axis):
    peers = lax.axis_size(axis)
    return lax.all_to_all(jnp.broadcast_to(x[None], (peers, *x.shape)), axis, 0, 0, tiled=True)


def of_everyone(x, axis):
    everything = sent_to_all(x, axis)
    return jnp.sum(everything, axis=0)


def cut_along(x, dim, peers):
    before, after = (x.shape[:dim], x.shape[dim + 1 :])
    return jnp.moveaxis(x.reshape(*before, peers, -1, *after), dim, 0)


def sum_at_owner(x, axis, dim):
    peers = lax.axis_size(axis)
    pieces = lax.all_to_all(cut_along(x, dim, peers), axis, 0, 0, tiled=True)
    return jnp.sum(pieces, axis=0)


def sum_in_two_steps(x, axes, dim):
    far, near = axes
    own = sum_at_owner(cut_along(x, dim, lax.axis_size(far)), near, dim + 1)
    return jnp.sum(lax.all_to_all(own, far, 0, 0, tiled=True), axis=0)


def one_axis_at_a_time(x, axes):
    for axis in axes:
        x = lax.psum(x, axis)
    return x


def mixing(sequence, state_weight, step_weight, step_bias, decay_log):
    state_width = state_weight.shape[1] // 2
    projected = jnp.dot(sequence, state_weight, preferred_element_type=jnp.float32)
    b_coef = projected[:, :state_width]
    c_coef = projected[:, state_width:]
    gram_matrix = jnp.dot(c_coef, b_coef.T, precision=lax.Precision.HIGHEST)
    step_size = jax.nn.softplus(
        jnp.dot(sequence, step_weight, preferred_element_type=jnp.float32) + step_bias
    )
    rate_step = jnp.exp(decay_log) * step_size
    cumulative = jnp.cumsum(rate_step, axis=0).T
    length = sequence.shape[0]
    row_later = lax.broadcasted_iota(jnp.int32, (length, length), 0)
    earlier = lax.broadcasted_iota(jnp.int32, (length, length), 1)
    causal = row_later >= earlier
    log_decay = cumulative[:, None, :] - cumulative[:, :, None]
    decay_matrix = jnp.where(causal[None], jnp.exp(jnp.minimum(log_decay, 0.0)), 0.0)
    return (gram_matrix[None] * decay_matrix * step_size.T[:, None, :]).astype(jnp.bfloat16)


def contract_rows(left, right):
    return lax.dot_general(
        left, right, (((0,), (0,)), ((), ())), preferred_element_type=jnp.float32
    )


def on_device(
    tokens,
    teacher,
    inner_weight,
    output_weight,
    inner_first,
    inner_second,
    state_weight,
    step_weight,
    step_bias,
    decay_log,
    skip_gain,
):
    seq_rows, model_width = tokens.shape
    heads_here = step_weight.shape[1]
    groups_here = inner_weight.shape[1] // HEAD_DIM
    ratio = HEADS // GROUPS
    total_tokens = seq_rows * lax.axis_size(DP)
    inner_full, output_full = sent_together(
        (inner_weight.astype(jnp.bfloat16), output_weight), DP, 0, 1
    )
    weights_mix = mixing(tokens, state_weight, step_weight, step_bias, decay_log)
    projected = jnp.dot(tokens, inner_full, preferred_element_type=jnp.float32).astype(jnp.bfloat16)
    heads_in = jnp.repeat(projected.reshape(seq_rows, groups_here, HEAD_DIM), ratio, axis=1)
    mixed = jnp.einsum(
        "hts,shp->thp", weights_mix, heads_in, preferred_element_type=jnp.float32
    ) + skip_gain[None, :, None] * heads_in.astype(jnp.float32)
    inner = mixed.astype(jnp.bfloat16).reshape(seq_rows, heads_here * HEAD_DIM)
    partial_out = lax.dot_general(
        inner, output_full, (((1,), (1,)), ((), ())), preferred_element_type=jnp.float32
    )
    student = of_everyone(partial_out, "tensor")
    error_rows = student - teacher.astype(jnp.float32)
    square_sum = jnp.where(lax.axis_index("tensor") == 0, jnp.sum(error_rows * error_rows), 0.0)
    grad_out = error_rows.astype(jnp.bfloat16)
    grad_inner = jnp.dot(grad_out, output_full, preferred_element_type=jnp.float32).astype(
        jnp.bfloat16
    )
    grad_heads = grad_inner.reshape(seq_rows, heads_here, HEAD_DIM)
    back = jnp.einsum(
        "hts,thp->shp", weights_mix, grad_heads, preferred_element_type=jnp.float32
    ) + skip_gain[None, :, None] * grad_heads.astype(jnp.float32)
    grouped = jnp.sum(back.reshape(seq_rows, groups_here, ratio, HEAD_DIM), axis=2)
    grad_projected = grouped.astype(jnp.bfloat16).reshape(seq_rows, groups_here * HEAD_DIM)
    inner_grad = sum_in_two_steps(
        contract_rows(tokens, grad_projected), (("dp_0", "dp_1", "dp_2"), "dp_3"), 0
    )
    local_squares = jnp.sum(inner_grad * inner_grad)
    squares_total, error_total = (
        one_axis_at_a_time(local_squares, DP_TENSOR),
        one_axis_at_a_time(square_sum, DP_TENSOR),
    )
    entry_count = model_width * groups_here * HEAD_DIM * lax.axis_size("tensor")
    root_mean = jnp.sqrt(squares_total / entry_count)
    factor = jnp.minimum(1.0, 1.0 / (root_mean + norm_eps))
    distill_loss = error_total / (total_tokens * model_width)
    first_fix = 1.0 - beta_one**STEP
    second_fix = 1.0 - beta_two**STEP
    clipped = factor * inner_grad
    first_next = beta_one * inner_first + (1.0 - beta_one) * clipped
    second_next = beta_two * inner_second + (1.0 - beta_two) * clipped * clipped
    update = (
        first_next / first_fix / (jnp.sqrt(second_next / second_fix) + adam_eps)
        + weight_decay * inner_weight
    )
    return (distill_loss, update, first_next, second_next)


def solution(mesh):
    finer = Mesh(
        mesh.devices.reshape(8, 4, 2, 2, mesh.shape["tensor"]),
        ("dp_0", "dp_1", "dp_2", "dp_3", "tensor"),
    )
    return jax.shard_map(
        on_device,
        mesh=finer,
        in_specs=(
            P(DP, None),
            P(DP, None),
            P(DP, "tensor"),
            P(DP, "tensor"),
            P(DP, "tensor"),
            P(DP, "tensor"),
            P(),
            P(None, "tensor"),
            P("tensor"),
            P("tensor"),
            P("tensor"),
        ),
        out_specs=(P(), P(DP, "tensor"), P(DP, "tensor"), P(DP, "tensor")),
        check_vma=False,
    )
```

profile of v0, /device:TPU:1, one launch (start us, length us, event | category | flops | bytes accessed | tf_op | source)
XLA Modules:
  0.0 278.1 jit_solution(4933198831317484721)
XLA Ops:
  7.2 0.8 convert_element_type.37
  8.0 1.4 pad_maximum_fusion
  9.4 0.7 exp.13
  10.1 1.0 compare_select_fusion
  11.3 0.2 reduce_window_sum.11
  11.5 1.2 fusion.25
  12.7 0.3 fusion.14
  13.0 124.1 %all-gather.2.cloned.1.call-done = bf16[2048,1280]{1,0:T(8,128)(2,1)} async-done(((bf16[16,1280]{1,0:T(8,128)(2,1)}), bf16[2048,1280]{1,0:T(8,128)(2,1)}) %all-gather.2.cloned.1.call-update) | async-done | bytes 5242896 | tf_op jit(solution)/shard_map/all_gather | solution.py:25
  137.1 1.7 convolution_convert_fusion
  138.9 1.0 fusion.9
  139.9 3.7 %fusion.2 = f32[128,2048]{1,0:T(8,128)S(1)} fusion(bf16[128,1024]{0,1:T(8,128)(2,1)S(1)} %bitcast.59, bf16[2048,1280]{1,0:T(8,128)(2,1)} %all-gather.2.cloned.1.call-done), kind=kOutput, calls=%fused_computation.2 | convolution fusion | flops 536870912 | bytes 5505024 | tf_op jit(solution)/shard_map/dot_general | solution.py:116
  143.6 0.2 broadcast_in_dim.16
  143.9 27.3 %all_to_all.15 = f32[2,128,2048]{2,1,0:T(8,128)S(1)} all-to-all(f32[2,128,2048]{2,1,0:T(8,128)S(1)} %broadcast_in_dim.16), channel_id=1, replica_groups=mesh['dp_0'=8,'dp_1'=4,'dp_2'=2,'dp_3'=2,'tensor'=2] {'tensor'}, dimensions={0} | all-to-all | bytes 4194304 | tf_op jit(solution)/shard_map/all_to_all | solution.py:31
  171.2 1.2 reduce_sum.54
  172.5 3.2 %fusion.6 = bf16[128,1024]{1,0:T(8,128)(2,1)S(1)} fusion(bf16[2048,1280]{1,0:T(8,128)(2,1)} %all-gather.2.cloned.1.call-done, f32[128,2048]{1,0:T(8,128)} %reduce_sum.54, bf16[128,2048]{1,0:T(8,128)(2,1)S(1)} %copy-done.1), kind=kOutput, calls=%fused_computation.9 | convolution fusion | flops 537788416 | bytes 6029312 | tf_op jit(solution)/shard_map/dot_general | solution.py:123
  175.7 0.2 copy.33
  175.9 0.4 bitcast_reduce_fusion
  176.3 0.4 convolution_bitcast_fusion
  176.7 1.9 copy.34
  178.6 1.8 copy.35
  180.4 6.2 %all_to_all.16 = f32[2,64,16,256]{3,2,1,0:T(8,128)S(1)} all-to-all(f32[2,64,16,256]{3,2,1,0:T(8,128)S(1)} %copy.35), channel_id=1, replica_groups=mesh['dp_0'=8,'dp_1'=4,'dp_2'=2,'dp_3'=2,'tensor'=2] {'dp_3'}, dimensions={0} | all-to-all | bytes 4194304 | tf_op jit(solution)/shard_map/all_to_all | solution.py:46
  186.6 1.3 reduce_sum.57
  187.8 7.8 %all-to-all-start.2 = ((f32[64,16,256]{2,1,0:T(8,128)}), f32[64,16,256]{2,1,0:T(8,128)S(1)}, u32[]{:S(2)}, u32[]{:S(2)}) async-start(f32[64,16,256]{2,1,0:T(8,128)} %reduce_sum.57), calls=%async_computation.2 | async-start | bytes 2097152 | tf_op jit(solution)/shard_map/all_to_all | solution.py:53
  195.7 2.1 multiply_reduce_fusion
  198.4 25.0 %all-to-all-done.2 = f32[64,16,256]{2,1,0:T(8,128)S(1)} async-done(((f32[64,16,256]{2,1,0:T(8,128)}), f32[64,16,256]{2,1,0:T(8,128)S(1)}, u32[]{:S(2)}, u32[]{:S(2)}) %all-to-all-start.2) | async-done | bytes 1048608 | tf_op jit(solution)/shard_map/all_to_all | solution.py:53
  223.5 0.6 multiply_reduce_fusion.1
  224.1 14.2 %all-reduce = (f32[]{:T(128)}, f32[]{:T(128)}) all-reduce(f32[]{:T(128)S(6)} %select_n.18, f32[]{:T(128)} %multiply_reduce_fusion.1), channel_id=1, replica_groups=mesh['dp_0'=8,'dp_1'=4,'dp_2'=2,'dp_3'=2,'tensor'=2] {'dp_0'}, use_global_device_ids=true, to_apply=%region_3.4 | all-reduce | flops 2 | bytes 16 | tf_op jit(solution)/shard_map/psum | solution.py:58
  238.3 7.5 %all-reduce.1 = (f32[]{:T(128)}, f32[]{:T(128)}) all-reduce(f32[]{:T(128)} %get-tuple-element.4, f32[]{:T(128)} %get-tuple-element.5), channel_id=1, replica_groups=mesh['dp_0'=8,'dp_1'=4,'dp_2'=2,'dp_3'=2,'tensor'=2] {'dp_1'}, use_global_device_ids=true, to_apply=%region_4.5 | all-reduce | flops 2 | bytes 16 | tf_op jit(solution)/shard_map/psum | solution.py:58
  245.8 5.9 %all-reduce.4 = (f32[]{:T(128)}, f32[]{:T(128)}) all-reduce(f32[]{:T(128)} %get-tuple-element.6, f32[]{:T(128)} %get-tuple-element.7), channel_id=1, replica_groups=mesh['dp_0'=8,'dp_1'=4,'dp_2'=2,'dp_3'=2,'tensor'=2] {'dp_2'}, use_global_device_ids=true, to_apply=%region_5.6 | all-reduce | flops 2 | bytes 16 | tf_op jit(solution)/shard_map/psum | solution.py:58
  251.7 11.9 %all-reduce.3 = (f32[]{:T(128)}, f32[]{:T(128)}) all-reduce(f32[]{:T(128)} %get-tuple-element.12, f32[]{:T(128)} %get-tuple-element.13), channel_id=1, replica_groups=mesh['dp_0'=8,'dp_1'=4,'dp_2'=2,'dp_3'=2,'tensor'=2] {'dp_3'}, use_global_device_ids=true, to_apply=%region_6.7 | all-reduce | flops 2 | bytes 16 | tf_op jit(solution)/shard_map/psum | solution.py:58
  263.6 4.4 %all-reduce.2 = (f32[]{:T(128)}, f32[]{:T(128)}) all-reduce(f32[]{:T(128)} %get-tuple-element.10, f32[]{:T(128)} %get-tuple-element.11), channel_id=1, replica_groups=mesh['dp_0'=8,'dp_1'=4,'dp_2'=2,'dp_3'=2,'tensor'=2] {'tensor'}, use_global_device_ids=true, to_apply=%region_7.8 | all-reduce | flops 2 | bytes 16 | tf_op jit(solution)/shard_map/psum | solution.py:58
  269.4 0.6 multiply_add_fusion
  (20 shorter events, 0.5 us)
Async XLA Ops:
  7.2 2.9 %copy-start = (bf16[128,2048]{1,0:T(8,128)(2,1)S(1)}, bf16[128,2048]{1,0:T(8,128)(2,1)}, u32[]{:S(2)}) copy-start(bf16[128,2048]{1,0:T(8,128)(2,1)} %param.11) | copy-start | bytes 1572868
  7.2 129.9 %all-gather.2.cloned.1.call-start = ((), (), s32[]{:S(2)}) async-start(), calls=%async_computation.3 | async-start | bytes 5283840 | tf_op jit(solution)/shard_map/all_gather | solution.py:25
  143.9 28.6 %copy-start.1 = (bf16[128,2048]{1,0:T(8,128)(2,1)S(1)}, bf16[128,2048]{1,0:T(8,128)(2,1)}, u32[]{:S(2)}) copy-start(bf16[128,2048]{1,0:T(8,128)(2,1)} %param.12) | copy-start | bytes 1572868
  172.5 3.4 %copy-start.5 = (f32[8]{0:T(128)S(1)}, f32[8]{0:T(128)}, u32[]{:S(2)}) copy-start(f32[8]{0:T(128)} %param.21) | copy-start | bytes 100
  186.6 82.9 %copy-start.2 = (f32[16,256]{1,0:T(8,128)S(1)}, f32[16,256]{1,0:T(8,128)}, u32[]{:S(2)}) copy-start(f32[16,256]{1,0:T(8,128)} %param.13) | copy-start | bytes 49156
  186.6 82.9 %copy-start.3 = (f32[16,256]{1,0:T(8,128)S(1)}, f32[16,256]{1,0:T(8,128)}, u32[]{:S(2)}) copy-start(f32[16,256]{1,0:T(8,128)} %param.15) | copy-start | bytes 49156
  186.6 82.9 %copy-start.4 = (f32[16,256]{1,0:T(8,128)S(1)}, f32[16,256]{1,0:T(8,128)}, u32[]{:S(2)}) copy-start(f32[16,256]{1,0:T(8,128)} %param.16) | copy-start | bytes 49156
  187.8 35.6 %all-to-all-start.2 = ((f32[64,16,256]{2,1,0:T(8,128)}), f32[64,16,256]{2,1,0:T(8,128)S(1)}, u32[]{:S(2)}, u32[]{:S(2)}) async-start(f32[64,16,256]{2,1,0:T(8,128)} %reduce_sum.57), calls=%async_computation.2 | async-start | bytes 2097152 | tf_op jit(solution)/shard_map/all_to_all | solution.py:53
Sparse Core Ops, SparseCore 0:
  11.6 125.4 all-gather.1
where the time goes:
time: 279 us; the launch traced here: 278 us
  waiting for transfers between devices  149 us (53%)
  blocking collectives  77.4 us (28%)
  between operations  17.4 us (6%)
  matrix products  13 us (5%)
  other arithmetic  8.35 us (3%)
  starting transfers between devices  7.89 us (3%)
  local copies, waits for them, and re-layouts  4.93 us (2%)
    all_gather x1, waiting for transfers between devices, sent_together(): whole = lax.all_gather(both, axis, axis=dim, tiled=True)  124 us
    psum x5, blocking collectives, one_axis_at_a_time(): x = lax.psum(x, axis)  43.9 us
    all_to_all x1, blocking collectives, sent_to_all(): lax.all_to_all(jnp.broadcast_to(x[None], (peers, *x.shape)), axis, 0, 0,...  27.3 us
    all_to_all x1, waiting for transfers between devices, sum_in_two_steps(): return jnp.sum(lax.all_to_all(own, far, 0, 0, tiled=True), axis=0)  25 us
    all_to_all x1, starting transfers between devices, sum_in_two_steps(): return jnp.sum(lax.all_to_all(own, far, 0, 0, tiled=True), axis=0)  7.85 us
    all_to_all x1, blocking collectives, sum_at_owner(): pieces = lax.all_to_all(cut_along(x, dim, peers), axis, 0, 0, tiled=True)  6.16 us
  transfers between devices with their start and end apart: 2, of which 2 were waited for; matrix products, arithmetic and copies ran while one was open for 2% of the time, Pallas kernels for 0%

commit v1 on v0

--- a/solution.py
+++ b/solution.py
@@ -1,6 +1,11 @@
+import functools
+import heapq
+
 import jax
 import jax.numpy as jnp
 from jax import lax
+from jax.experimental import pallas as pl
+from jax.experimental.pallas import tpu as pltpu
 from jax.sharding import Mesh
 from jax.sharding import PartitionSpec as P
 
@@ -19,11 +24,143 @@
 norm_eps = 1e-06
 
 
-def sent_together(arrays, axis, dim, along):
-    widths = [a.shape[along] for a in arrays]
-    both = jnp.concatenate(arrays, axis=along)
-    whole = lax.all_gather(both, axis, axis=dim, tiled=True)
-    return tuple(jnp.split(whole, [sum(widths[:k]) for k in range(1, len(widths))], axis=along))
+SIZES = {"dp_0": 8, "dp_1": 4, "dp_2": 2}
+
+
+def relay_plan(order, sizes, wire=0.88, latency=1.8):
+    def direction(rel, k):
+        n, v = sizes[order[k]], rel[k]
+        if n == 2:
+            return 1
+        if 2 * v == n:
+            return 1 if sum(rel[:k]) % 2 == 0 else -1
+        return 1 if 2 * v < n else -1
+
+    def children(rel):
+        last = max([k for k in range(3) if rel[k]], default=-1)
+        out = []
+        if last >= 0 and sizes[order[last]] > 2:
+            sign = direction(rel, last)
+            n = sizes[order[last]]
+            nxt = list(rel)
+            nxt[last] = (rel[last] + sign) % n
+            steps_now = rel[last] if sign > 0 else n - rel[last]
+            steps_nxt = nxt[last] if sign > 0 else n - nxt[last]
+            if nxt[last] and steps_nxt == steps_now + 1 and direction(nxt, last) == sign:
+                out.append((last, sign, tuple(nxt)))
+        for k in range(last + 1, 3):
+            n = sizes[order[k]]
+            for sign in (1, -1) if n > 2 else (1,):
+                nxt = list(rel)
+                nxt[k] = sign % n
+                out.append((k, sign, tuple(nxt)))
+        return out
+
+    root = (0, 0, 0)
+    free = {}
+    ready = [(0.0, root)]
+    steps = []
+    while ready:
+        now, rel = heapq.heappop(ready)
+        sends = children(rel)
+        steps.append((now, rel, sends))
+        for k, sign, nxt in sends:
+            begin = max(now, free.get((k, sign), 0.0))
+            free[(k, sign)] = begin + wire
+            heapq.heappush(ready, (begin + wire + latency + (0.8 if sizes[order[k]] == 2 else 0), nxt))
+    return steps
+
+
+TORUS = ("dp_0", "dp_1", "dp_2")
+ORDERS = (("dp_2", "dp_1", "dp_0"), ("dp_2", "dp_0", "dp_1"))
+
+
+def enter_with(peers):
+    barrier = pltpu.get_barrier_semaphore()
+    for peer in peers:
+        pl.semaphore_signal(barrier, inc=1, device_id=peer, device_id_type=pl.DeviceIdType.MESH)
+    pl.semaphore_wait(barrier, len(peers))
+
+
+def gather_kernel(sizes, mine, out, send_sem, recv_sem, pair_sem):
+    here = {a: lax.axis_index(a) for a in TORUS}
+    core = lax.axis_index("dp_3")
+
+    def shifted(axis, by):
+        return lax.rem(here[axis] + (by % sizes[axis]), sizes[axis])
+
+    other = {"dp_3": 1 - core}
+    neighbours = [{a: shifted(a, s)} for a in TORUS for s in ((1, -1) if sizes[a] > 2 else (1,))]
+    enter_with(neighbours + [other])
+
+    def relay(order, core_id):
+        def slot(rel):
+            at = {a: shifted(a, -v) for a, v in zip(order, rel)}
+            return ((at["dp_0"] * sizes["dp_1"] + at["dp_1"]) * sizes["dp_2"] + at["dp_2"]) * 2 + core_id
+
+        def number(rel):
+            return (rel[0] * sizes[order[1]] + rel[1]) * sizes[order[2]] + rel[2]
+
+        for _, rel, sends in relay_plan(order, sizes):
+            own = not any(rel)
+            where = slot(rel)
+            block = mine if own else out.at[where]
+            if not own:
+                pltpu.make_async_remote_copy(
+                    out.at[where], out.at[where], send_sem, recv_sem.at[number(rel)],
+                    device_id=other, device_id_type=pl.DeviceIdType.MESH,
+                ).wait_recv()
+            for k, sign, nxt in sends:
+                pltpu.make_async_remote_copy(
+                    block, out.at[where], send_sem, recv_sem.at[number(nxt)],
+                    device_id={order[k]: shifted(order[k], sign)},
+                    device_id_type=pl.DeviceIdType.MESH,
+                ).start()
+            pltpu.make_async_remote_copy(
+                block, out.at[where], send_sem, pair_sem,
+                device_id=other, device_id_type=pl.DeviceIdType.MESH,
+            ).start()
+            if own:
+                out[where] = mine[...]
+
+    @pl.when(core == 0)
+    def _():
+        relay(ORDERS[0], 0)
+
+    @pl.when(core == 1)
+    def _():
+        relay(ORDERS[1], 1)
+
+    pieces = sizes["dp_0"] * sizes["dp_1"] * sizes["dp_2"]
+    pltpu.make_async_remote_copy(
+        out.at[pl.ds(0, pieces)], out.at[pl.ds(0, pieces)], send_sem, pair_sem,
+        device_id=other, device_id_type=pl.DeviceIdType.MESH,
+    ).wait_recv()
+    sent = 2 * pieces - 1
+    pltpu.make_async_remote_copy(
+        out.at[pl.ds(0, sent)], out.at[pl.ds(0, sent)], send_sem, pair_sem,
+        device_id=other, device_id_type=pl.DeviceIdType.MESH,
+    ).wait_send()
+
+
+def gathered(mine):
+    sizes = {a: lax.axis_size(a) for a in TORUS}
+    pieces = sizes["dp_0"] * sizes["dp_1"] * sizes["dp_2"]
+    return pl.pallas_call(
+        functools.partial(gather_kernel, sizes),
+        name="gather",
+        out_shape=jax.ShapeDtypeStruct((2 * pieces, *mine.shape), mine.dtype),
+        in_specs=[pl.BlockSpec(memory_space=pltpu.VMEM)],
+        out_specs=pl.BlockSpec(memory_space=pltpu.VMEM),
+        scratch_shapes=[
+            pltpu.SemaphoreType.DMA,
+            pltpu.SemaphoreType.DMA((pieces,)),
+            pltpu.SemaphoreType.DMA,
+        ],
+        compiler_params=pltpu.CompilerParams(
+            collective_id=0, has_side_effects=True, vmem_limit_bytes=16 * 1024 * 1024
+        ),
+    )(mine)
 
 
 def sent_to_all(x, axis):
@@ -51,12 +188,6 @@
     far, near = axes
     own = sum_at_owner(cut_along(x, dim, lax.axis_size(far)), near, dim + 1)
     return jnp.sum(lax.all_to_all(own, far, 0, 0, tiled=True), axis=0)
-
-
-def one_axis_at_a_time(x, axes):
-    for axis in axes:
-        x = lax.psum(x, axis)
-    return x
 
 
 def mixing(sequence, state_weight, step_weight, step_bias, decay_log):
@@ -103,9 +234,9 @@
     groups_here = inner_weight.shape[1] // HEAD_DIM
     ratio = HEADS // GROUPS
     total_tokens = seq_rows * lax.axis_size(DP)
-    inner_full, output_full = sent_together(
-        (inner_weight.astype(jnp.bfloat16), output_weight), DP, 0, 1
-    )
+    whole = gathered(jnp.concatenate([inner_weight.astype(jnp.bfloat16), output_weight], axis=1))
+    whole = whole.reshape(model_width, whole.shape[-1])
+    inner_full, output_full = jnp.split(whole, [inner_weight.shape[1]], axis=1)
     weights_mix = mixing(tokens, state_weight, step_weight, step_bias, decay_log)
     projected = jnp.dot(tokens, inner_full, preferred_element_type=jnp.float32).astype(jnp.bfloat16)
     heads_in = jnp.repeat(projected.reshape(seq_rows, groups_here, HEAD_DIM), ratio, axis=1)
@@ -133,10 +264,7 @@
         contract_rows(tokens, grad_projected), (("dp_0", "dp_1", "dp_2"), "dp_3"), 0
     )
     local_squares = jnp.sum(inner_grad * inner_grad)
-    squares_total, error_total = (
-        one_axis_at_a_time(local_squares, DP_TENSOR),
-        one_axis_at_a_time(square_sum, DP_TENSOR),
-    )
+    squares_total, error_total = lax.psum(jnp.stack([local_squares, square_sum]), DP_TENSOR)
     entry_count = model_width * groups_here * HEAD_DIM * lax.axis_size("tensor")
     root_mean = jnp.sqrt(squares_total / entry_count)
     factor = jnp.minimum(1.0, 1.0 / (root_mean + norm_eps))

time: 279 us -> 208 us (0.75)
  waiting for transfers between devices: 149 us -> 25 us
  Pallas kernels: 0 us -> 35.7 us
  blocking collectives: 77.4 us -> 109 us
  between operations: 17.4 us -> 4.05 us
  matrix products: 13 us -> 9.47 us
    all_gather x1 -> x0, waiting for transfers between devices: 124 us -> none  [sent_together(): whole = lax.all_gather(both, axis, axis=dim, tiled=True)]
    pallas_call x0 -> x1, Pallas kernels: none -> 35.7 us  [gathered(): pl.pallas_call(functools.partial(gather_kernel, sizes), name='gather', ou...]
    psum x5 -> x1, blocking collectives: 43.9 us -> 75.4 us  [on_device(): lax.psum(jnp.stack([local_squares, square_sum]), DP_TENSOR)]
  transfers between devices with their start and end apart: 2 -> 1, of which waited for: 2 -> 1; matrix products, arithmetic and copies ran while one was open for 2% -> 1% of each run, Pallas kernels for 0% -> 0%
where the time goes in v1:
time: 208 us; the launch traced here: 207 us
  blocking collectives  109 us (52%)
  Pallas kernels  35.7 us (17%)
  waiting for transfers between devices  25 us (12%)
  matrix products  9.47 us (5%)
  other arithmetic  8.45 us (4%)
  starting transfers between devices  8.43 us (4%)
  local copies, waits for them, and re-layouts  7.16 us (3%)
  between operations  4.05 us (2%)
    psum x1, blocking collectives, on_device(): lax.psum(jnp.stack([local_squares, square_sum]), DP_TENSOR)  75.4 us
    pallas_call x1, Pallas kernels, gathered(): pl.pallas_call(functools.partial(gather_kernel, sizes), name='gather', ou...  35.7 us
    all_to_all x1, blocking collectives, sent_to_all(): lax.all_to_all(jnp.broadcast_to(x[None], (peers, *x.shape)), axis, 0, 0,...  27.4 us
    all_to_all x1, waiting for transfers between devices, sum_in_two_steps(): return jnp.sum(lax.all_to_all(own, far, 0, 0, tiled=True), axis=0)  25 us
    all_to_all x1, starting transfers between devices, sum_in_two_steps(): return jnp.sum(lax.all_to_all(own, far, 0, 0, tiled=True), axis=0)  8.43 us
    all_to_all x1, blocking collectives, sum_at_owner(): pieces = lax.all_to_all(cut_along(x, dim, peers), axis, 0, 0, tiled=True)  6.06 us
  transfers between devices with their start and end apart: 1, of which 1 were waited for; matrix products, arithmetic and copies ran while one was open for 1% of the time, Pallas kernels for 0%

profile of v1, /device:TPU:1, one launch (start us, length us, event | category | flops | bytes accessed | tf_op | source)
XLA Modules:
  0.0 207.2 jit_solution(11444684607515960984)
XLA Ops:
  0.7 0.8 convert_element_type.37
  1.5 0.8 pad_maximum_fusion.mine
  2.2 35.7 %gather.1 = bf16[128,16,1280]{2,1,0:T(8,128)(2,1)S(1)} custom-call(bf16[16,1280]{1,0:T(8,128)(2,1)S(1)} %pad_maximum_fusion.mine), custom_call_target="tpu_custom_call" | custom-call | tf_op jit(solution)/shard_map/gather/pallas_call | solution.py:149
  38.0 2.3 %copy-done.1 = bf16[128,16,1280]{2,1,0:T(8,128)(2,1)} copy-done((bf16[128,16,1280]{2,1,0:T(8,128)(2,1)}, bf16[128,16,1280]{2,1,0:T(8,128)(2,1)S(1)}, u32[]{:S(2)}) %copy-start.1) | copy-done | bytes 5242904
  40.3 0.5 convolution_convert_fusion
  40.8 0.2 compare_select_fusion
  41.1 0.1 copy.30
  41.3 0.2 reduce_window_sum.11
  41.5 0.3 fusion.26
  41.8 0.3 fusion.14
  42.1 0.4 fusion.9
  42.5 3.7 %fusion.2 = f32[128,2048]{1,0:T(8,128)S(1)} fusion(bf16[128,1024]{0,1:T(8,128)(2,1)S(1)} %bitcast.67, bf16[2048,1280]{1,0:T(8,128)(2,1)} %bitcast.59), kind=kOutput, calls=%fused_computation.2 | convolution fusion | flops 536870912 | bytes 5505024 | tf_op jit(solution)/shard_map/dot_general | solution.py:247
  46.3 0.2 broadcast_in_dim.16
  46.5 27.4 %all_to_all.15 = f32[2,128,2048]{2,1,0:T(8,128)S(1)} all-to-all(f32[2,128,2048]{2,1,0:T(8,128)S(1)} %broadcast_in_dim.16), channel_id=1, replica_groups=mesh['dp_0'=8,'dp_1'=4,'dp_2'=2,'dp_3'=2,'tensor'=2] {'tensor'}, dimensions={0} | all-to-all | bytes 4194304 | tf_op jit(solution)/shard_map/all_to_all | solution.py:168
  74.0 1.2 reduce_sum.54
  75.2 3.2 %fusion.6 = bf16[128,1024]{1,0:T(8,128)(2,1)S(1)} fusion(bf16[2048,1280]{1,0:T(8,128)(2,1)} %bitcast.60, f32[128,2048]{1,0:T(8,128)} %reduce_sum.54, bf16[128,2048]{1,0:T(8,128)(2,1)S(1)} %copy-done.2), kind=kOutput, calls=%fused_computation.9 | convolution fusion | flops 537788416 | bytes 6029312 | tf_op jit(solution)/shard_map/dot_general | solution.py:254
  78.5 0.2 copy.33
  78.6 0.4 bitcast_reduce_fusion
  79.0 0.4 convolution_bitcast_fusion
  79.5 1.9 copy.34
  81.3 1.8 copy.35
  83.1 6.1 %all_to_all.16 = f32[2,64,16,256]{3,2,1,0:T(8,128)S(1)} all-to-all(f32[2,64,16,256]{3,2,1,0:T(8,128)S(1)} %copy.35), channel_id=1, replica_groups=mesh['dp_0'=8,'dp_1'=4,'dp_2'=2,'dp_3'=2,'tensor'=2] {'dp_3'}, dimensions={0} | all-to-all | bytes 4194304 | tf_op jit(solution)/shard_map/all_to_all | solution.py:183
  89.2 1.3 reduce_sum.56
  90.4 8.4 %all-to-all-start.2 = ((f32[64,16,256]{2,1,0:T(8,128)}), f32[64,16,256]{2,1,0:T(8,128)S(1)}, u32[]{:S(2)}, u32[]{:S(2)}) async-start(f32[64,16,256]{2,1,0:T(8,128)} %reduce_sum.56), calls=%async_computation.2 | async-start | bytes 2097152 | tf_op jit(solution)/shard_map/all_to_all | solution.py:190
  98.9 2.1 %multiply_reduce_fusion = f32[]{:T(128)} fusion(f32[128,2048]{1,0:T(8,128)} %reduce_sum.54, bf16[128,2048]{1,0:T(8,128)(2,1)S(1)} %copy-done.2), kind=kLoop, calls=%fused_computation.14 | loop fusion | flops 1048575 | bytes 1572868 | tf_op jit(solution)/shard_map/reduce_sum | solution.py:252
  101.6 25.0 %all-to-all-done.2 = f32[64,16,256]{2,1,0:T(8,128)S(1)} async-done(((f32[64,16,256]{2,1,0:T(8,128)}), f32[64,16,256]{2,1,0:T(8,128)S(1)}, u32[]{:S(2)}, u32[]{:S(2)}) %all-to-all-start.2) | async-done | bytes 1048608 | tf_op jit(solution)/shard_map/all_to_all | solution.py:190
  126.6 0.1 reduce_sum.57
  126.7 0.6 multiply_reduce_fusion.1
  127.3 0.7 pad_maximum_fusion.1
  128.0 75.4 %psum.7 = f32[2]{0:T(128)S(1)} all-reduce(f32[2]{0:T(128)S(1)} %pad_maximum_fusion.1), channel_id=1, replica_groups=mesh['dp_0'=8,'dp_1'=4,'dp_2'=2,'dp_3'=2,'tensor'=2] {'dp_0','dp_1','dp_..., use_global_device_ids=true, to_apply=%region_7.8 | all-reduce | flops 2 | bytes 16 | tf_op jit(solution)/shard_map/psum | solution.py:267
  203.4 0.6 fusion.25
  205.4 0.6 multiply_add_fusion
  (26 shorter events, 0.2 us)
Async XLA Ops:
  0.6 39.7 %copy-start = (bf16[128,2048]{1,0:T(8,128)(2,1)S(1)}, bf16[128,2048]{1,0:T(8,128)(2,1)}, u32[]{:S(2)}) copy-start(bf16[128,2048]{1,0:T(8,128)(2,1)} %param.11) | copy-start | bytes 1572868
  0.6 37.3 %copy-start.9 = (f32[8]{0:T(128)S(1)}, f32[8]{0:T(128)}, u32[]{:S(2)}) copy-start(f32[8]{0:T(128)} %param.20) | copy-start | bytes 100
  0.7 40.1 %copy-start.5 = (bf16[2048,8]{0,1:T(8,128)(2,1)S(1)}, bf16[2048,8]{0,1:T(8,128)(2,1)}, u32[]{:S(2)}) copy-start(bf16[2048,8]{0,1:T(8,128)(2,1)} %param.18) | copy-start | bytes 98308
  0.7 40.1 %copy-start.8 = (f32[8]{0:T(128)S(1)}, f32[8]{0:T(128)}, u32[]{:S(2)}) copy-start(f32[8]{0:T(128)} %param.19) | copy-start | bytes 100
  0.7 40.8 %copy-start.3 = (bf16[2048,32]{0,1:T(8,128)(2,1)S(1)}, bf16[2048,32]{0,1:T(8,128)(2,1)}, u32[]{:S(2)}) copy-start(bf16[2048,32]{0,1:T(8,128)(2,1)} %param.17) | copy-start | bytes 393220
  2.2 39.9 %copy-start.10 = (f32[8]{0:T(128)S(1)}, f32[8]{0:T(128)}, u32[]{:S(2)}) copy-start(f32[8]{0:T(128)} %param.21) | copy-start | bytes 100
  38.0 2.3 %copy-start.1 = (bf16[128,16,1280]{2,1,0:T(8,128)(2,1)}, bf16[128,16,1280]{2,1,0:T(8,128)(2,1)S(1)}, u32[]{:S(2)}) copy-start(bf16[128,16,1280]{2,1,0:T(8,128)(2,1)S(1)} %gather.1) | copy-start | bytes 15728644
  46.5 28.7 %copy-start.2 = (bf16[128,2048]{1,0:T(8,128)(2,1)S(1)}, bf16[128,2048]{1,0:T(8,128)(2,1)}, u32[]{:S(2)}) copy-start(bf16[128,2048]{1,0:T(8,128)(2,1)} %param.12) | copy-start | bytes 1572868
  89.2 116.2 %copy-start.4 = (f32[16,256]{1,0:T(8,128)S(1)}, f32[16,256]{1,0:T(8,128)}, u32[]{:S(2)}) copy-start(f32[16,256]{1,0:T(8,128)} %param.13) | copy-start | bytes 49156
  89.2 116.2 %copy-start.6 = (f32[16,256]{1,0:T(8,128)S(1)}, f32[16,256]{1,0:T(8,128)}, u32[]{:S(2)}) copy-start(f32[16,256]{1,0:T(8,128)} %param.15) | copy-start | bytes 49156
  89.2 116.2 %copy-start.7 = (f32[16,256]{1,0:T(8,128)S(1)}, f32[16,256]{1,0:T(8,128)}, u32[]{:S(2)}) copy-start(f32[16,256]{1,0:T(8,128)} %param.16) | copy-start | bytes 49156
  90.4 36.1 %all-to-all-start.2 = ((f32[64,16,256]{2,1,0:T(8,128)}), f32[64,16,256]{2,1,0:T(8,128)S(1)}, u32[]{:S(2)}, u32[]{:S(2)}) async-start(f32[64,16,256]{2,1,0:T(8,128)} %reduce_sum.56), calls=%async_computation.2 | async-start | bytes 2097152 | tf_op jit(solution)/shard_map/all_to_all | solution.py:190

commit v2 on v1

--- a/solution.py
+++ b/solution.py
@@ -163,31 +163,223 @@
     )(mine)
 
 
-def sent_to_all(x, axis):
-    peers = lax.axis_size(axis)
-    return lax.all_to_all(jnp.broadcast_to(x[None], (peers, *x.shape)), axis, 0, 0, tiled=True)
-
-
-def of_everyone(x, axis):
-    everything = sent_to_all(x, axis)
-    return jnp.sum(everything, axis=0)
-
-
-def cut_along(x, dim, peers):
-    before, after = (x.shape[:dim], x.shape[dim + 1 :])
-    return jnp.moveaxis(x.reshape(*before, peers, -1, *after), dim, 0)
-
-
-def sum_at_owner(x, axis, dim):
-    peers = lax.axis_size(axis)
-    pieces = lax.all_to_all(cut_along(x, dim, peers), axis, 0, 0, tiled=True)
-    return jnp.sum(pieces, axis=0)
-
-
-def sum_in_two_steps(x, axes, dim):
-    far, near = axes
-    own = sum_at_owner(cut_along(x, dim, lax.axis_size(far)), near, dim + 1)
-    return jnp.sum(lax.all_to_all(own, far, 0, 0, tiled=True), axis=0)
+CHUNK = 256
+
+
+def step_kernel(
+    sizes, inner, weight, tokens, teacher, mix, skip, grad_out, sums_out,
+    tok_t, tok_all, mix_t, part, leaving, arrived, grad_acc, gp_all, g_part, g_all, row_a, row_b,
+    student_send, student_recv, tok_send, tok_recv, gp_send, gp_recv,
+    g_send, g_recv, a_send, a_recv, b_send, b_recv,
+):
+    axes = ("dp_0", "dp_1", "dp_2", "dp_3", "tensor")
+    here = {a: lax.axis_index(a) for a in axes}
+    nz, nx, ny = sizes["dp_0"], sizes["dp_1"], sizes["dp_2"]
+    features, cols = weight.shape
+    chunks = features // CHUNK
+    head_dim = mix.shape[-1]
+    groups = gp_all.shape[-1] // head_dim
+    per_group = cols // head_dim // groups
+
+    def there(**by):
+        return {
+            a: lax.rem(here[a] + v, sizes[a]) for a, v in by.items() if v % sizes[a]
+        }
+
+    def remote(src, dst, send, recv, target):
+        return pltpu.make_async_remote_copy(
+            src, dst, send, recv, device_id=target, device_id_type=pl.DeviceIdType.MESH
+        )
+
+    plane = [
+        dict(dp_1=i, dp_2=j, dp_3=k, tensor=t)
+        for i in range(nx) for j in range(ny) for k in range(2) for t in range(2)
+    ][1:]
+    column = [dict(dp_0=i, dp_2=j) for i in range(nz) for j in range(ny)][1:]
+    peers = plane + [by for by in column if by["dp_0"]]
+    barrier = pltpu.get_barrier_semaphore()
+    for by in peers:
+        pl.semaphore_signal(
+            barrier, inc=1, device_id=there(**by), device_id_type=pl.DeviceIdType.MESH
+        )
+
+    other_half = there(tensor=1)
+
+    def student_copy(i):
+        return remote(
+            leaving.at[i], arrived.at[i], student_send, student_recv.at[i], other_half
+        )
+
+    for i in range(chunks):
+        rows = weight[pl.ds(i * CHUNK, CHUNK), :]
+        piece = lax.dot_general(
+            inner[...], rows, (((1,), (1,)), ((), ())), preferred_element_type=jnp.float32
+        )
+        part[i] = piece
+        leaving[i] = piece.astype(jnp.bfloat16)
+        if i == 0:
+            pl.semaphore_wait(barrier, len(peers))
+        else:
+            student_copy(i - 1).start()
+    student_copy(chunks - 1).start()
+
+    seq = tokens.shape[0]
+    for k in range(features // 128):
+        turned = tokens[:, k * 128 : (k + 1) * 128].T
+        per = tok_t.shape[4]
+        tok_t[k * 128 // (nx * ny * 2 * per), (k * 128 // (ny * 2 * per)) % nx : (k * 128 // (ny * 2 * per)) % nx + 128 // (ny * 2 * per)] = (
+            turned.reshape(128 // (ny * 2 * per), ny, 2, per, seq)
+        )
+    tok_sends = []
+    for i in range(nx):
+        for k in range(2):
+            slot = i * 2 + k
+            to_x = lax.rem(here["dp_1"] + i, nx)
+            to_c = lax.rem(here["dp_3"] + k, 2)
+            if slot:
+                tok_sends.append((slot, to_x, to_c, there(dp_1=i, dp_3=k)))
+    for slot, to_x, to_c, target in tok_sends:
+        remote(
+            tok_t.at[:, to_x, :, to_c], tok_all.at[slot], tok_send, tok_recv, target
+        ).start()
+    tok_all[0] = tok_t[:, here["dp_1"], :, here["dp_3"]]
+    for g in range(groups):
+        for h in range(per_group):
+            mix_t[g, :, h * seq : (h + 1) * seq] = mix[g * per_group + h].T
+
+    squares = jnp.zeros((8, CHUNK), jnp.float32)
+    for i in range(chunks):
+        student_copy(i).wait_recv()
+        error = (
+            part[i] + arrived[i].astype(jnp.float32)
+            - teacher[:, i * CHUNK : (i + 1) * CHUNK].astype(jnp.float32)
+        )
+        squares = squares + jnp.sum((error * error).reshape(seq // 8, 8, CHUNK), axis=0)
+        product = jnp.dot(
+            error.astype(jnp.bfloat16), weight[pl.ds(i * CHUNK, CHUNK), :],
+            preferred_element_type=jnp.float32,
+        )
+        if i == 0:
+            grad_acc[...] = product
+        else:
+            grad_acc[...] += product
+    for g in range(groups):
+        heads = []
+        direct = None
+        for h in range(per_group):
+            at = slice((g * per_group + h) * head_dim, (g * per_group + h + 1) * head_dim)
+            one = grad_acc[:, at].astype(jnp.bfloat16)
+            heads.append(one)
+            term = skip[:, at] * one.astype(jnp.float32)
+            direct = term if direct is None else direct + term
+        back = jnp.dot(
+            mix_t[g], jnp.concatenate(heads, axis=0), preferred_element_type=jnp.float32
+        )
+        gp_all[0, :, g * head_dim : (g + 1) * head_dim] = (back + direct).astype(jnp.bfloat16)
+
+    pair = there(dp_3=1)
+    for i in (2, 1, 3) if nx == 4 else range(1, nx):
+        remote(
+            gp_all.at[0], gp_all.at[2 * i], gp_send, gp_recv.at[2 * i], there(dp_1=i)
+        ).start()
+    remote(gp_all.at[0], gp_all.at[1], gp_send, gp_recv.at[1], pair).start()
+    members = 2 * nx
+    block = tok_all.at[0]
+    remote(
+        tok_all.at[pl.ds(1, members - 1)], tok_all.at[pl.ds(1, members - 1)],
+        tok_send, tok_recv, pair,
+    ).wait()
+
+    def product_of(slot):
+        left = tok_all[slot].reshape(-1, seq)
+        return jnp.dot(left, gp_all[slot], preferred_element_type=jnp.float32)
+
+    remote(gp_all.at[1], gp_all.at[1], gp_send, gp_recv.at[1], pair).wait_recv()
+    total = product_of(0) + product_of(1)
+    order = (1, 3, 2) if nx == 4 else range(1, nx)
+    for i in order:
+        remote(gp_all.at[0], gp_all.at[2 * i], gp_send, gp_recv.at[2 * i], pair).wait_recv()
+        remote(
+            gp_all.at[2 * i], gp_all.at[2 * i + 1], gp_send, gp_recv.at[2 * i + 1], pair
+        ).start()
+        total = total + product_of(2 * i)
+    for i in order:
+        remote(
+            gp_all.at[0], gp_all.at[2 * i + 1], gp_send, gp_recv.at[2 * i + 1], pair
+        ).wait_recv()
+        total = total + product_of(2 * i + 1)
+    g_part[...] = total.reshape(g_part.shape)
+
+    for by in sorted(column, key=lambda b: -min(b["dp_0"], nz - b["dp_0"]) - b["dp_2"]):
+        slot = by["dp_0"] * ny + by["dp_2"]
+        to_z = lax.rem(here["dp_0"] + by["dp_0"], nz)
+        to_y = lax.rem(here["dp_2"] + by["dp_2"], ny)
+        remote(g_part.at[to_z, to_y], g_all.at[slot], g_send, g_recv, there(**by)).start()
+    g_all[0] = g_part[here["dp_0"], here["dp_2"]]
+    err = jnp.sum(squares) * 0.5
+    rest = g_all.at[pl.ds(1, nz * ny - 1)]
+    remote(rest, rest, g_send, g_recv, pair).wait()
+    grad = jnp.sum(g_all[...], axis=0)
+    grad_out[...] = grad
+    lane = lax.broadcasted_iota(jnp.int32, (1, 128), 1)
+    row = jnp.where(lane == 0, jnp.sum(grad * grad), jnp.where(lane == 1, err, 0.0))
+    row_a[0] = row
+    for n, by in enumerate(plane):
+        remote(row_a.at[0], row_a.at[n + 1], a_send, a_recv, there(**by)).start()
+    rest = row_a.at[pl.ds(1, len(plane))]
+    remote(rest, rest, a_send, a_recv, pair).wait()
+    row_b[0] = jnp.sum(row_a[...], axis=0)
+    for i in range(1, nz):
+        remote(row_b.at[0], row_b.at[i], b_send, b_recv, there(dp_0=i)).start()
+    rest = row_b.at[pl.ds(1, nz - 1)]
+    remote(rest, rest, b_send, b_recv, pair).wait()
+    sums_out[...] = jnp.sum(row_b[...], axis=0)
+
+    rest = gp_all.at[pl.ds(1, members - 1)]
+    remote(rest, rest, gp_send, gp_recv.at[1], pair).wait_send()
+    remote(leaving, leaving, student_send, student_recv.at[0], pair).wait_send()
+
+
+def after_gather(inner, weight, tokens, teacher, mix, skip, own_rows):
+    sizes = {a: lax.axis_size(a) for a in ("dp_0", "dp_1", "dp_2", "dp_3", "tensor")}
+    nz, nx, ny = sizes["dp_0"], sizes["dp_1"], sizes["dp_2"]
+    seq, features = tokens.shape
+    cols = weight.shape[1]
+    chunks = features // CHUNK
+    heads = mix.shape[0]
+    gcols = GROUPS // sizes["tensor"] * HEAD_DIM
+    f32, half = jnp.float32, jnp.bfloat16
+    vmem = pl.BlockSpec(memory_space=pltpu.VMEM)
+    dma = pltpu.SemaphoreType.DMA
+    return pl.pallas_call(
+        functools.partial(step_kernel, sizes),
+        name="after_gather",
+        out_shape=(
+            jax.ShapeDtypeStruct((own_rows, gcols), f32),
+            jax.ShapeDtypeStruct((1, 128), f32),
+        ),
+        in_specs=[vmem] * 6,
+        out_specs=(vmem, vmem),
+        scratch_shapes=[
+            pltpu.VMEM((nz, nx, ny, 2, own_rows, seq), half),
+            pltpu.VMEM((2 * nx, nz, ny, own_rows, seq), half),
+            pltpu.VMEM((gcols // HEAD_DIM, seq, heads * HEAD_DIM * seq // gcols), half),
+            pltpu.VMEM((chunks, seq, CHUNK), f32),
+            pltpu.VMEM((chunks, seq, CHUNK), half),
+            pltpu.VMEM((chunks, seq, CHUNK), half),
+            pltpu.VMEM((seq, cols), f32),
+            pltpu.VMEM((2 * nx, seq, gcols), half),
+            pltpu.VMEM((nz, ny, own_rows, gcols), f32),
+            pltpu.VMEM((nz * ny, own_rows, gcols), f32),
+            pltpu.VMEM((nx * ny * 4, 1, 128), f32),
+            pltpu.VMEM((nz, 1, 128), f32),
+            dma, dma((chunks,)), dma, dma, dma, dma((2 * nx,)),
+            dma, dma, dma, dma, dma, dma,
+        ],
+        compiler_params=pltpu.CompilerParams(
+            collective_id=1, has_side_effects=True, vmem_limit_bytes=32 * 1024 * 1024
+        ),
+    )(inner, weight, tokens, teacher, mix, skip)
 
 
 def mixing(sequence, state_weight, step_weight, step_bias, decay_log):
@@ -208,12 +400,6 @@
     log_decay = cumulative[:, None, :] - cumulative[:, :, None]
     decay_matrix = jnp.where(causal[None], jnp.exp(jnp.minimum(log_decay, 0.0)), 0.0)
     return (gram_matrix[None] * decay_matrix * step_size.T[:, None, :]).astype(jnp.bfloat16)
-
-
-def contract_rows(left, right):
-    return lax.dot_general(
-        left, right, (((0,), (0,)), ((), ())), preferred_element_type=jnp.float32
-    )
 
 
 def on_device(
@@ -244,27 +430,11 @@
         "hts,shp->thp", weights_mix, heads_in, preferred_element_type=jnp.float32
     ) + skip_gain[None, :, None] * heads_in.astype(jnp.float32)
     inner = mixed.astype(jnp.bfloat16).reshape(seq_rows, heads_here * HEAD_DIM)
-    partial_out = lax.dot_general(
-        inner, output_full, (((1,), (1,)), ((), ())), preferred_element_type=jnp.float32
+    inner_grad, sums = after_gather(
+        inner, output_full, tokens, teacher, weights_mix,
+        jnp.repeat(skip_gain, HEAD_DIM)[None, :], inner_weight.shape[0],
     )
-    student = of_everyone(partial_out, "tensor")
-    error_rows = student - teacher.astype(jnp.float32)
-    square_sum = jnp.where(lax.axis_index("tensor") == 0, jnp.sum(error_rows * error_rows), 0.0)
-    grad_out = error_rows.astype(jnp.bfloat16)
-    grad_inner = jnp.dot(grad_out, output_full, preferred_element_type=jnp.float32).astype(
-        jnp.bfloat16
-    )
-    grad_heads = grad_inner.reshape(seq_rows, heads_here, HEAD_DIM)
-    back = jnp.einsum(
-        "hts,thp->shp", weights_mix, grad_heads, preferred_element_type=jnp.float32
-    ) + skip_gain[None, :, None] * grad_heads.astype(jnp.float32)
-    grouped = jnp.sum(back.reshape(seq_rows, groups_here, ratio, HEAD_DIM), axis=2)
-    grad_projected = grouped.astype(jnp.bfloat16).reshape(seq_rows, groups_here * HEAD_DIM)
-    inner_grad = sum_in_two_steps(
-        contract_rows(tokens, grad_projected), (("dp_0", "dp_1", "dp_2"), "dp_3"), 0
-    )
-    local_squares = jnp.sum(inner_grad * inner_grad)
-    squares_total, error_total = lax.psum(jnp.stack([local_squares, square_sum]), DP_TENSOR)
+    squares_total, error_total = sums[0, 0], sums[0, 1]
     entry_count = model_width * groups_here * HEAD_DIM * lax.axis_size("tensor")
     root_mean = jnp.sqrt(squares_total / entry_count)
     factor = jnp.minimum(1.0, 1.0 / (root_mean + norm_eps))

time: 208 us -> 92.4 us (0.44)
  blocking collectives: 109 us -> 0 us
  Pallas kernels: 35.7 us -> 78.5 us
  waiting for transfers between devices: 25 us -> 0 us
  starting transfers between devices: 8.43 us -> 0 us
  matrix products: 9.47 us -> 1.71 us
  other arithmetic: 8.45 us -> 2.64 us
    psum x1 -> x0, blocking collectives: 75.4 us -> none  [on_device(): lax.psum(jnp.stack([local_squares, square_sum]), DP_TENSOR)]
    pallas_call x0 -> x1, Pallas kernels: none -> 42.7 us  [after_gather(): pl.pallas_call(functools.partial(step_kernel, sizes), name='after_gather'...]
    all_to_all x2 -> x0, blocking collectives: 33.5 us -> none  [the longest x1 27.4 us: sent_to_all(): lax.all_to_all(jnp.broadcast_to(x[None], (peers, *x.shape)), axis, 0, 0,...]
    all_to_all x1 -> x0, waiting for transfers between devices: 25 us -> none  [sum_in_two_steps(): return jnp.sum(lax.all_to_all(own, far, 0, 0, tiled=True), axis=0)]
    all_to_all x1 -> x0, starting transfers between devices: 8.43 us -> none  [sum_in_two_steps(): return jnp.sum(lax.all_to_all(own, far, 0, 0, tiled=True), axis=0)]
    dot_general x4 -> x0, matrix products: 7.76 us -> none  [the longest x1 3.72 us: on_device(): lax.dot_general(inner, output_full, (((1,), (1,)), ((), ())), preferred_e...]
    reduce_sum x5 -> x0, other arithmetic: 5.3 us -> none  [the longest x1 2.1 us: on_device(): jnp.sum(error_rows * error_rows)]
    split x0 -> x1, local copies, waits for them, and re-layouts: none -> 2.64 us  [on_device(): inner_full, output_full = jnp.split(whole, [inner_weight.shape[1]], axis=1)]
  transfers between devices with their start and end apart: 1 -> 0, of which waited for: 1 -> 0; matrix products, arithmetic and copies ran while one was open for 1% -> 0% of each run, Pallas kernels for 0% -> 0%
where the time goes in v2:
time: 92.4 us; the launch traced here: 92.2 us
  Pallas kernels  78.5 us (85%)
  local copies, waits for them, and re-layouts  5.99 us (6%)
  between operations  3.39 us (4%)
  other arithmetic  2.64 us (3%)
  matrix products  1.71 us (2%)
    pallas_call x1, Pallas kernels, after_gather(): pl.pallas_call(functools.partial(step_kernel, sizes), name='after_gather'...  42.7 us
    pallas_call x1, Pallas kernels, gathered(): pl.pallas_call(functools.partial(gather_kernel, sizes), name='gather', ou...  35.7 us
    split x1, local copies, waits for them, and re-layouts, on_device(): inner_full, output_full = jnp.split(whole, [inner_weight.shape[1]], axis=1)  2.64 us
    unnamed x22, local copies, waits for them, and re-layouts  2.35 us

profile of v2, /device:TPU:1, one launch (start us, length us, event | category | flops | bytes accessed | tf_op | source)
XLA Modules:
  0.0 92.2 jit_solution(13109285366253195957)
XLA Ops:
  0.6 0.0 copy-start
  0.6 0.0 copy-start.2
  0.7 0.0 copy-start.9
  0.7 0.0 copy-start.8
  0.7 0.0 copy-start.5
  0.7 0.0 copy-start.10
  0.7 0.8 convert_element_type.18
  1.5 0.8 pad_maximum_fusion.mine
  2.2 35.7 %gather.1 = bf16[128,16,1280]{2,1,0:T(8,128)(2,1)S(1)} custom-call(bf16[16,1280]{1,0:T(8,128)(2,1)S(1)} %pad_maximum_fusion.mine), custom_call_target="tpu_custom_call" | custom-call | tf_op jit(solution)/shard_map/gather/pallas_call | solution.py:149
  38.0 0.0 copy-start.1
  38.0 2.3 %copy-done.1 = bf16[128,16,1280]{2,1,0:T(8,128)(2,1)} copy-done((bf16[128,16,1280]{2,1,0:T(8,128)(2,1)}, bf16[128,16,1280]{2,1,0:T(8,128)(2,1)S(1)}, u32[]{:S(2)}) %copy-start.1) | copy-done | bytes 5242904
  40.3 0.5 convolution_convert_fusion
  40.8 0.2 compare_select_fusion
  41.1 0.0 copy-done.10
  41.1 0.1 fusion.7
  41.2 0.1 copy.15
  41.3 0.2 reduce_window_sum.11
  41.5 0.0 copy-done
  41.5 0.3 fusion.14
  41.8 0.3 fusion.4
  42.2 0.0 copy-start.3
  42.2 0.4 fusion.1
  42.6 0.1 copy.19.inner
  42.7 0.0 copy-start.4
  42.7 0.0 copy-start.6
  42.7 0.0 copy-start.7
  42.7 2.6 %split.9.weight = bf16[2048,1024]{1,0:T(8,128)(2,1)S(1)} slice(bf16[2048,1280]{1,0:T(8,128)(2,1)} %bitcast.39), slice={[0:2048], [256:1280]} | slice | bytes 8388608 | tf_op jit(solution)/shard_map/split | solution.py:425
  45.4 0.2 multiply_convert_fusion.mix
  45.6 0.1 broadcast_in_dim.16
  45.7 42.7 %after_gather.1 = (f32[16,256]{1,0:T(8,128)S(1)}, f32[1,128]{1,0:T(1,128)S(1)}) custom-call(bf16[128,1024]{1,0:T(8,128)(2,1)S(1)} %copy.19.inner, bf16[2048,1024]{1,0:T(8,128)(2,1)S(1)} %split.9.weight, bf16[128,2048]{1,0:T(8,128)(2,1)S(1)} %copy-done.2, bf16[128,2048]{1,0:T(8,128)(2,1)S(1)} %copy-done.3, bf16[8,128,128]{2,1,0:T(8,128)(2,1)S(1)} %multiply_convert_fusion.mix, ...), custom_call_target="tpu_custom_call" | custom-call | tf_op jit(solution)/shard_map/after_gather/pallas_call | solution.py:354
  88.4 0.6 fusion.13
  90.4 0.6 multiply_add_fusion
  (12 shorter events, 0.1 us)
Async XLA Ops:
  0.6 40.9 %copy-start = (bf16[2048,32]{0,1:T(8,128)(2,1)S(1)}, bf16[2048,32]{0,1:T(8,128)(2,1)}, u32[]{:S(2)}) copy-start(bf16[2048,32]{0,1:T(8,128)(2,1)} %param.17) | copy-start | bytes 393220
  0.6 39.6 %copy-start.2 = (bf16[128,2048]{1,0:T(8,128)(2,1)S(1)}, bf16[128,2048]{1,0:T(8,128)(2,1)}, u32[]{:S(2)}) copy-start(bf16[128,2048]{1,0:T(8,128)(2,1)} %tokens.1) | copy-start | bytes 1572868
  0.7 41.5 %copy-start.9 = (f32[8]{0:T(128)S(1)}, f32[8]{0:T(128)}, u32[]{:S(2)}) copy-start(f32[8]{0:T(128)} %param.21) | copy-start | bytes 100
  0.7 40.1 %copy-start.8 = (f32[8]{0:T(128)S(1)}, f32[8]{0:T(128)}, u32[]{:S(2)}) copy-start(f32[8]{0:T(128)} %param.19) | copy-start | bytes 100
  0.7 40.1 %copy-start.5 = (bf16[2048,8]{0,1:T(8,128)(2,1)S(1)}, bf16[2048,8]{0,1:T(8,128)(2,1)}, u32[]{:S(2)}) copy-start(bf16[2048,8]{0,1:T(8,128)(2,1)} %param.18) | copy-start | bytes 98308
  0.7 40.4 %copy-start.10 = (f32[8]{0:T(128)S(1)}, f32[8]{0:T(128)}, u32[]{:S(2)}) copy-start(f32[8]{0:T(128)} %param.20) | copy-start | bytes 100
  38.0 2.3 %copy-start.1 = (bf16[128,16,1280]{2,1,0:T(8,128)(2,1)}, bf16[128,16,1280]{2,1,0:T(8,128)(2,1)S(1)}, u32[]{:S(2)}) copy-start(bf16[128,16,1280]{2,1,0:T(8,128)(2,1)S(1)} %gather.1) | copy-start | bytes 15728644
  42.2 3.5 %copy-start.3 = (bf16[128,2048]{1,0:T(8,128)(2,1)S(1)}, bf16[128,2048]{1,0:T(8,128)(2,1)}, u32[]{:S(2)}) copy-start(bf16[128,2048]{1,0:T(8,128)(2,1)} %teacher.1) | copy-start | bytes 1572868
  42.7 47.7 %copy-start.4 = (f32[16,256]{1,0:T(8,128)S(1)}, f32[16,256]{1,0:T(8,128)}, u32[]{:S(2)}) copy-start(f32[16,256]{1,0:T(8,128)} %param.13) | copy-start | bytes 49156
  42.7 47.7 %copy-start.6 = (f32[16,256]{1,0:T(8,128)S(1)}, f32[16,256]{1,0:T(8,128)}, u32[]{:S(2)}) copy-start(f32[16,256]{1,0:T(8,128)} %param.15) | copy-start | bytes 49156
  42.7 47.7 %copy-start.7 = (f32[16,256]{1,0:T(8,128)S(1)}, f32[16,256]{1,0:T(8,128)}, u32[]{:S(2)}) copy-start(f32[16,256]{1,0:T(8,128)} %param.16) | copy-start | bytes 49156

commit v3 on v2

v3 whole, which is shorter than its diff:
```python
import functools
import heapq

import jax
import jax.numpy as jnp
from jax import lax
from jax.experimental import pallas as pl
from jax.experimental.pallas import tpu as pltpu
from jax.sharding import Mesh
from jax.sharding import PartitionSpec as P

HEAD_DIM = 128
STEP = 20
DP = ("dp_0", "dp_1", "dp_2", "dp_3")


beta_one = 0.9
beta_two = 0.95
adam_eps = 1e-08
weight_decay = 0.1
norm_eps = 1e-06


TORUS = ("dp_0", "dp_1", "dp_2")
BY_COLUMN = ("dp_2", "dp_1", "dp_0")
BY_ROW = ("dp_2", "dp_0", "dp_1")
CHUNK = 256


def ways(sizes):
    def sign(rel, order):
        n, v = sizes[order[2]], rel[order[2]]
        if 2 * v == n:
            return 1 if (rel[order[0]] + rel[order[1]]) % 2 == 0 else -1
        return 1 if 2 * v < n else -1

    def onward(rel, order):
        last = order[2]
        n = sizes[last]
        if rel[last] == 0:
            moves = [1, -1] if n > 2 else [1]
        else:
            moves = [sign(rel, order)]
        out = []
        for move in moves:
            nxt = dict(rel)
            nxt[last] = (rel[last] + move) % n
            far = nxt[last] if move > 0 else n - nxt[last]
            was = rel[last] if move > 0 else (n - rel[last]) % n
            if nxt[last] and far == was + 1 and (n == 2 or sign(nxt, order) == move):
                out.append(nxt)
        return out

    def children(rel, order):
        out = onward(rel, order)
        if not any(rel.values()):
            for i in range(sizes[order[0]]):
                for j in range(sizes[order[1]]):
                    if i or j:
                        out.append({order[0]: i, order[1]: j, order[2]: 0})
            out.sort(key=lambda r: -sum(min(v, sizes[a] - v) for a, v in r.items()))
        return out

    return children


def relay_times(sizes, flows, latency=2.45, hop=0.45):
    children = ways(sizes)
    free, heap, count = {}, [], 0
    events = [[] for _ in flows]
    for n, (order, wire, start) in enumerate(flows):
        heapq.heappush(heap, (start, count, n, {a: 0 for a in TORUS}))
        count += 1
    while heap:
        now, _, n, rel = heapq.heappop(heap)
        order, wire, _ = flows[n]
        sends = children(rel, order)
        events[n].append((now, rel, sends))
        for nxt in sends:
            lands, hops = now, 0
            for a in TORUS:
                v = (nxt[a] - rel[a]) % sizes[a]
                if v:
                    go = 1 if 2 * v <= sizes[a] else -1
                    far = min(v, sizes[a] - v) * (2 if sizes[a] == 2 else 1)
                    begin = max(now, free.get((a, go), 0.0))
                    free[(a, go)] = begin + wire * far
                    lands = max(lands, begin + wire)
                    hops += far
            heapq.heappush(heap, (lands + latency + hop * (hops - 1), count, n, nxt))
            count += 1
    return events


def step_kernel(
    sizes, tokens, teacher, inner_weight, output_weight, state_weight, step_weight,
    step_bias, decay_log, skip, grad_out, sums_out,
    mine, in_all, w_all, mix, mix_t, inner,
    tok_t, tok_all, part, leaving, arrived, grad_acc, gp_all, g_part, g_all, row_a, row_b,
    in_send, in_recv, in_pair, w_send, w_recv, w_pair,
    student_send, student_recv, tok_send, tok_recv, gp_send, gp_recv,
    g_send, g_recv, a_send, a_recv, b_send, b_recv,
):
    axes = ("dp_0", "dp_1", "dp_2", "dp_3", "tensor")
    here = {a: lax.axis_index(a) for a in axes}
    nz, nx, ny = sizes["dp_0"], sizes["dp_1"], sizes["dp_2"]
    seq, features = tokens.shape
    cols = output_weight.shape[1]
    chunks = features // CHUNK
    heads = mix.shape[0]
    head_dim = cols // heads
    groups = inner_weight.shape[1] // head_dim
    per_group = heads // groups
    core = here["dp_3"]

    def ahead(a, v):
        return lax.rem(here[a] + (v % sizes[a]), sizes[a])

    def there(**by):
        return {a: ahead(a, v) for a, v in by.items() if v % sizes[a]}

    def remote(src, dst, send, recv, target):
        return pltpu.make_async_remote_copy(
            src, dst, send, recv, device_id=target, device_id_type=pl.DeviceIdType.MESH
        )

    plane = [
        dict(dp_1=i, dp_2=j, dp_3=k, tensor=t)
        for i in range(nx) for j in range(ny) for k in range(2) for t in range(2)
    ][1:]
    column = [dict(dp_0=i, dp_2=j) for i in range(nz) for j in range(ny)][1:]
    peers = plane + [by for by in column if by["dp_0"]]
    pair = there(dp_3=1)
    barrier = pltpu.get_barrier_semaphore()
    for by in peers:
        pl.semaphore_signal(
            barrier, inc=1, device_id=there(**by), device_id_type=pl.DeviceIdType.MESH
        )
    mine[...] = inner_weight[...].astype(jnp.bfloat16)
    in_all[here["dp_0"], here["dp_1"], here["dp_2"], core] = mine[...]
    w_all[here["dp_0"], here["dp_1"], here["dp_2"], core] = output_weight[...]

    in_wire, w_wire = 0.088, 0.352
    flows = (
        (BY_ROW, in_wire, 0.0), (BY_ROW, in_wire, 0.0),
        (BY_COLUMN, w_wire, 0.01), (BY_ROW, w_wire, 0.01),
    )
    events = relay_times(sizes, flows)
    steps = [
        sorted(
            [(t, 0, rel, sends) for t, rel, sends in events[c]]
            + [(t, 1, rel, sends) for t, rel, sends in events[2 + c]],
            key=lambda e: e[:2],
        )
        for c in range(2)
    ]

    def number(rel):
        return (rel["dp_0"] * nx + rel["dp_1"]) * ny + rel["dp_2"]

    def relay(c, begin, end):
        for time, kind, rel, sends in steps[c]:
            if not begin <= time < end:
                continue
            all_ref, own, send, recv = (
                (in_all, mine, in_send, in_recv), (w_all, output_weight, w_send, w_recv)
            )[kind]
            at = tuple(ahead(a, -rel[a]) for a in TORUS)
            slot = all_ref.at[at[0], at[1], at[2], c]
            first = not any(rel.values())
            block = own if first else slot
            if not first:
                remote(slot, slot, send, recv.at[number(rel)], pair).wait_recv()
            for nxt in sends:
                target = there(**{a: nxt[a] - rel[a] for a in TORUS})
                remote(block, slot, send, recv.at[number(nxt)], target).start()
            beside = in_pair if kind == 0 else w_pair.at[rel["dp_0"]]
            remote(block, slot, send, beside, pair).start()

    def relay_until(begin, end):
        for c in range(2):
            @pl.when(core == c)
            def _():
                relay(c, begin, end)

    def turn_tokens():
        per = tok_t.shape[4]
        rows_x = ny * 2 * per
        for k in range(features // 128):
            turned = tokens[:, k * 128 : (k + 1) * 128].T
            z, x = divmod(k * 128 // rows_x, nx)
            tok_t[z, x : x + 128 // rows_x] = turned.reshape(128 // rows_x, ny, 2, per, seq)

    def mix_heads():
        projected = jnp.dot(tokens[...], state_weight[...], preferred_element_type=jnp.float32)
        width = projected.shape[1] // 2
        b_coef, c_coef = projected[:, :width], projected[:, width:]
        gram = lax.dot_general(
            c_coef, b_coef, (((1,), (1,)), ((), ())),
            precision=lax.Precision.HIGHEST, preferred_element_type=jnp.float32,
        )
        raw = (
            jnp.dot(tokens[...], step_weight[...], preferred_element_type=jnp.float32)
            + step_bias[...]
        )
        step_size = jnp.maximum(raw, 0.0) + jnp.log1p(jnp.exp(-jnp.abs(raw)))
        rate = jnp.exp(decay_log[...]) * step_size
        later = lax.broadcasted_iota(jnp.int32, (seq, seq), 0)
        earlier = lax.broadcasted_iota(jnp.int32, (seq, seq), 1)
        causal = later >= earlier
        cumulative = jnp.dot(
            causal.astype(jnp.float32), rate,
            precision=lax.Precision.HIGHEST, preferred_element_type=jnp.float32,
        )
        blank = jnp.zeros((seq, seq - heads), jnp.float32)
        cum_t = jnp.concatenate([cumulative, blank], axis=1).T
        step_t = jnp.concatenate([step_size, blank], axis=1).T
        for h in range(heads):
            log_decay = cum_t[h : h + 1, :] - cumulative[:, h : h + 1]
            decay = jnp.where(causal, jnp.exp(jnp.minimum(log_decay, 0.0)), 0.0)
            mix[h] = (gram * decay * step_t[h : h + 1, :]).astype(jnp.bfloat16)

    def turn_mix():
        for g in range(groups):
            for h in range(per_group):
                mix_t[g, :, h * seq : (h + 1) * seq] = mix[g * per_group + h].T

    def project():
        width = inner_weight.shape[1]
        projected = jnp.dot(
            tokens[...], in_all[...].reshape(features, width),
            preferred_element_type=jnp.float32,
        ).astype(jnp.bfloat16)
        for g in range(groups):
            source = projected[:, g * head_dim : (g + 1) * head_dim]
            stack = mix[g * per_group : (g + 1) * per_group].reshape(per_group * seq, seq)
            mixed = jnp.dot(stack, source, preferred_element_type=jnp.float32)
            wide = source.astype(jnp.float32)
            for h in range(per_group):
                n = g * per_group + h
                inner[:, n * head_dim : (n + 1) * head_dim] = (
                    mixed[h * seq : (h + 1) * seq] + skip[:, n : n + 1] * wide
                ).astype(jnp.bfloat16)

    other_half = there(tensor=1)
    order = sorted(range(nz), key=lambda v: (min(v, nz - v), v))

    def student_copy(i):
        return remote(
            leaving.at[i], arrived.at[i], student_send, student_recv.at[i], other_half
        )

    def w_rows(i):
        return w_all[ahead("dp_0", -order[i])].reshape(CHUNK, cols)

    def teacher_cols(i):
        return teacher[:, pl.ds(pl.multiple_of(ahead("dp_0", -order[i]) * CHUNK, CHUNK), CHUNK)]

    def student(i):
        beside = w_all.at[0, :, :, 0]
        remote(beside, beside, w_send, w_pair.at[order[i]], pair).wait_recv()
        piece = lax.dot_general(
            inner[...], w_rows(i), (((1,), (1,)), ((), ())), preferred_element_type=jnp.float32
        )
        part[i] = piece
        leaving[i] = piece.astype(jnp.bfloat16)
        if i:
            student_copy(i - 1).start()

    pl.semaphore_wait(barrier, len(peers))
    late = max(t for t, *_ in steps[0] + steps[1]) + 1
    inner_done = max(t for c in range(2) for t, kind, *_ in steps[c] if kind == 0) + 1e-6
    relay_until(0, 2.0)
    turn_tokens()
    relay_until(2.0, 6.0)
    mix_heads()
    relay_until(6.0, 9.0)
    turn_mix()
    relay_until(9.0, max(inner_done, 9.0))
    beside = in_all.at[:, :, :, 0]
    remote(beside, beside, in_send, in_pair, pair).wait_recv()
    project()
    reached = max(inner_done, 9.0)
    for i in range(chunks):
        needed = max(
            t for c in range(2) for t, kind, rel, _ in steps[c]
            if kind == 1 and rel["dp_0"] == order[i]
        ) + 1e-6
        if needed > reached:
            relay_until(reached, needed)
            reached = needed
        student(i)
    relay_until(reached, late)
    student_copy(chunks - 1).start()

    tok_sends = []
    for i in range(nx):
        for k in range(2):
            slot = i * 2 + k
            to_x = lax.rem(here["dp_1"] + i, nx)
            to_c = lax.rem(here["dp_3"] + k, 2)
            if slot:
                tok_sends.append((slot, to_x, to_c, there(dp_1=i, dp_3=k)))
    for slot, to_x, to_c, target in tok_sends:
        remote(
            tok_t.at[:, to_x, :, to_c], tok_all.at[slot], tok_send, tok_recv, target
        ).start()
    tok_all[0] = tok_t[:, here["dp_1"], :, here["dp_3"]]

    squares = jnp.zeros((8, CHUNK), jnp.float32)
    for i in range(chunks):
        student_copy(i).wait_recv()
        error = (
            part[i] + arrived[i].astype(jnp.float32)
            - teacher_cols(i).astype(jnp.float32)
        )
        squares = squares + jnp.sum((error * error).reshape(seq // 8, 8, CHUNK), axis=0)
        product = jnp.dot(
            error.astype(jnp.bfloat16), w_rows(i), preferred_element_type=jnp.float32,
        )
        if i == 0:
            grad_acc[...] = product
        else:
            grad_acc[...] += product
    for g in range(groups):
        heads = []
        direct = None
        for h in range(per_group):
            at = slice((g * per_group + h) * head_dim, (g * per_group + h + 1) * head_dim)
            one = grad_acc[:, at].astype(jnp.bfloat16)
            heads.append(one)
            n = g * per_group + h
            term = skip[:, n : n + 1] * one.astype(jnp.float32)
            direct = term if direct is None else direct + term
        back = jnp.dot(
            mix_t[g], jnp.concatenate(heads, axis=0), preferred_element_type=jnp.float32
        )
        gp_all[0, :, g * head_dim : (g + 1) * head_dim] = (back + direct).astype(jnp.bfloat16)

    for i in (2, 1, 3) if nx == 4 else range(1, nx):
        remote(
            gp_all.at[0], gp_all.at[2 * i], gp_send, gp_recv.at[2 * i], there(dp_1=i)
        ).start()
    remote(gp_all.at[0], gp_all.at[1], gp_send, gp_recv.at[1], pair).start()
    members = 2 * nx
    remote(
        tok_all.at[pl.ds(1, members - 1)], tok_all.at[pl.ds(1, members - 1)],
        tok_send, tok_recv, pair,
    ).wait()

    def product_of(slot):
        left = tok_all[slot].reshape(-1, seq)
        return jnp.dot(left, gp_all[slot], preferred_element_type=jnp.float32)

    remote(gp_all.at[1], gp_all.at[1], gp_send, gp_recv.at[1], pair).wait_recv()
    total = product_of(0) + product_of(1)
    near = (1, 3, 2) if nx == 4 else range(1, nx)
    for i in near:
        remote(gp_all.at[0], gp_all.at[2 * i], gp_send, gp_recv.at[2 * i], pair).wait_recv()
        remote(
            gp_all.at[2 * i], gp_all.at[2 * i + 1], gp_send, gp_recv.at[2 * i + 1], pair
        ).start()
        total = total + product_of(2 * i)
    for i in near:
        remote(
            gp_all.at[0], gp_all.at[2 * i + 1], gp_send, gp_recv.at[2 * i + 1], pair
        ).wait_recv()
        total = total + product_of(2 * i + 1)
    g_part[...] = total.reshape(g_part.shape)

    for by in sorted(column, key=lambda b: -min(b["dp_0"], nz - b["dp_0"]) - b["dp_2"]):
        slot = by["dp_0"] * ny + by["dp_2"]
        to_z = lax.rem(here["dp_0"] + by["dp_0"], nz)
        to_y = lax.rem(here["dp_2"] + by["dp_2"], ny)
        remote(g_part.at[to_z, to_y], g_all.at[slot], g_send, g_recv, there(**by)).start()
    g_all[0] = g_part[here["dp_0"], here["dp_2"]]
    err = jnp.sum(squares) * 0.5
    rest = g_all.at[pl.ds(1, nz * ny - 1)]
    remote(rest, rest, g_send, g_recv, pair).wait()
    grad = jnp.sum(g_all[...], axis=0)
    grad_out[...] = grad
    lane = lax.broadcasted_iota(jnp.int32, (1, 128), 1)
    row = jnp.where(lane == 0, jnp.sum(grad * grad), jnp.where(lane == 1, err, 0.0))
    row_a[0] = row
    for n, by in enumerate(plane):
        remote(row_a.at[0], row_a.at[n + 1], a_send, a_recv, there(**by)).start()
    rest = row_a.at[pl.ds(1, len(plane))]
    remote(rest, rest, a_send, a_recv, pair).wait()
    row_b[0] = jnp.sum(row_a[...], axis=0)
    for i in range(1, nz):
        remote(row_b.at[0], row_b.at[i], b_send, b_recv, there(dp_0=i)).start()
    rest = row_b.at[pl.ds(1, nz - 1)]
    remote(rest, rest, b_send, b_recv, pair).wait()
    sums_out[...] = jnp.sum(row_b[...], axis=0)

    rest = gp_all.at[pl.ds(1, members - 1)]
    remote(rest, rest, gp_send, gp_recv.at[1], pair).wait_send()
    remote(leaving, leaving, student_send, student_recv.at[0], pair).wait_send()
    pieces = nz * nx * ny
    for block, ref, send in (((0,), in_all, in_send), ((0,), w_all, w_send)):
        half = ref.at[:, :, :, 0]
        remote(half, half, send, in_pair, pair).wait_send()
        rest = ref.at[pl.ds(0, nz - 1), :, :, 0]
        remote(rest, rest, send, in_pair, pair).wait_send()
        rest = ref.at[0, pl.ds(0, nx - 1), :, 0]
        remote(rest, rest, send, in_pair, pair).wait_send()
        rest = ref.at[0, 0, pl.ds(0, ny - 1), 0]
        remote(rest, rest, send, in_pair, pair).wait_send()


def whole_step(
    tokens, teacher, inner_weight, output_weight, state_weight, step_weight,
    step_bias, decay_log, skip_gain,
):
    sizes = {a: lax.axis_size(a) for a in ("dp_0", "dp_1", "dp_2", "dp_3", "tensor")}
    nz, nx, ny = sizes["dp_0"], sizes["dp_1"], sizes["dp_2"]
    seq, features = tokens.shape
    own_rows, cols = output_weight.shape
    gcols = inner_weight.shape[1]
    heads = step_weight.shape[1]
    chunks = features // CHUNK
    groups = gcols // HEAD_DIM
    f32, half = jnp.float32, jnp.bfloat16
    vmem = pl.BlockSpec(memory_space=pltpu.VMEM)
    dma = pltpu.SemaphoreType.DMA
    return pl.pallas_call(
        functools.partial(step_kernel, sizes),
        name="whole_step",
        out_shape=(
            jax.ShapeDtypeStruct((own_rows, gcols), f32),
            jax.ShapeDtypeStruct((1, 128), f32),
        ),
        in_specs=[vmem] * 9,
        out_specs=(vmem, vmem),
        scratch_shapes=[
            pltpu.VMEM((own_rows, gcols), half),
            pltpu.VMEM((nz, nx, ny, 2, own_rows, gcols), half),
            pltpu.VMEM((nz, nx, ny, 2, own_rows, cols), half),
            pltpu.VMEM((heads, seq, seq), half),
            pltpu.VMEM((groups, seq, heads // groups * seq), half),
            pltpu.VMEM((seq, cols), half),
            pltpu.VMEM((nz, nx, ny, 2, own_rows, seq), half),
            pltpu.VMEM((2 * nx, nz, ny, own_rows, seq), half),
            pltpu.VMEM((chunks, seq, CHUNK), f32),
            pltpu.VMEM((chunks, seq, CHUNK), half),
            pltpu.VMEM((chunks, seq, CHUNK), half),
            pltpu.VMEM((seq, cols), f32),
            pltpu.VMEM((2 * nx, seq, gcols), half),
            pltpu.VMEM((nz, ny, own_rows, gcols), f32),
            pltpu.VMEM((nz * ny, own_rows, gcols), f32),
            pltpu.VMEM((nx * ny * 4, 1, 128), f32),
            pltpu.VMEM((nz, 1, 128), f32),
            dma, dma((nz * nx * ny,)), dma, dma, dma((nz * nx * ny,)), dma((nz,)),
            dma, dma((chunks,)), dma, dma, dma, dma((2 * nx,)),
            dma, dma, dma, dma, dma, dma,
        ],
        compiler_params=pltpu.CompilerParams(
            collective_id=0, has_side_effects=True, vmem_limit_bytes=40 * 1024 * 1024
        ),
    )(
        tokens, teacher, inner_weight, output_weight, state_weight, step_weight,
        step_bias[None, :], decay_log[None, :], skip_gain[None, :],
    )


def on_device(
    tokens,
    teacher,
    inner_weight,
    output_weight,
    inner_first,
    inner_second,
    state_weight,
    step_weight,
    step_bias,
    decay_log,
    skip_gain,
):
    seq_rows, model_width = tokens.shape
    groups_here = inner_weight.shape[1] // HEAD_DIM
    total_tokens = seq_rows * lax.axis_size(DP)
    inner_grad, sums = whole_step(
        tokens, teacher, inner_weight, output_weight, state_weight, step_weight,
        step_bias, decay_log, skip_gain,
    )
    squares_total, error_total = sums[0, 0], sums[0, 1]
    entry_count = model_width * groups_here * HEAD_DIM * lax.axis_size("tensor")
    root_mean = jnp.sqrt(squares_total / entry_count)
    factor = jnp.minimum(1.0, 1.0 / (root_mean + norm_eps))
    distill_loss = error_total / (total_tokens * model_width)
    first_fix = 1.0 - beta_one**STEP
    second_fix = 1.0 - beta_two**STEP
    clipped = factor * inner_grad
    first_next = beta_one * inner_first + (1.0 - beta_one) * clipped
    second_next = beta_two * inner_second + (1.0 - beta_two) * clipped * clipped
    update = (
        first_next / first_fix / (jnp.sqrt(second_next / second_fix) + adam_eps)
        + weight_decay * inner_weight
    )
    return (distill_loss, update, first_next, second_next)


def solution(mesh):
    finer = Mesh(
        mesh.devices.reshape(8, 4, 2, 2, mesh.shape["tensor"]),
        ("dp_0", "dp_1", "dp_2", "dp_3", "tensor"),
    )
    return jax.shard_map(
        on_device,
        mesh=finer,
        in_specs=(
            P(DP, None),
            P(DP, None),
            P(DP, "tensor"),
            P(DP, "tensor"),
            P(DP, "tensor"),
            P(DP, "tensor"),
            P(),
            P(None, "tensor"),
            P("tensor"),
            P("tensor"),
            P("tensor"),
        ),
        out_specs=(P(), P(DP, "tensor"), P(DP, "tensor"), P(DP, "tensor")),
        check_vma=False,
    )
```

time: 92.4 us -> 82.7 us (0.90)
  local copies, waits for them, and re-layouts: 5.99 us -> 2.95 us
  Pallas kernels: 78.5 us -> 75.6 us
  other arithmetic: 2.64 us -> 0.63 us
  matrix products: 1.71 us -> 0 us
    pallas_call x2 -> x1, Pallas kernels: 78.5 us -> 75.6 us  [whole_step(): pl.pallas_call(functools.partial(step_kernel, sizes), name='whole_step',...]
    split x1 -> x0, local copies, waits for them, and re-layouts: 2.64 us -> none  [on_device(): inner_full, output_full = jnp.split(whole, [inner_weight.shape[1]], axis=1)]
    dot_general x5 -> x0, matrix products: 1.71 us -> none  [the longest x1 0.48 us: on_device(): jnp.dot(tokens, inner_full, preferred_element_type=jnp.float32)]
    convert_element_type x2 -> x0, other arithmetic: 1 us -> none  [the longest x1 0.78 us: on_device(): inner_weight.astype(jnp.bfloat16)]
    unnamed x22 -> x20, local copies, waits for them, and re-layouts: 2.35 us -> 2.36 us
where the time goes in v3:
time: 82.7 us; the launch traced here: 82.5 us
  Pallas kernels  75.6 us (91%)
  between operations  3.31 us (4%)
  local copies, waits for them, and re-layouts  2.95 us (4%)
    pallas_call x1, Pallas kernels, whole_step(): pl.pallas_call(functools.partial(step_kernel, sizes), name='whole_step',...  75.6 us
    unnamed x20, local copies, waits for them, and re-layouts  2.36 us

profile of v3, /device:TPU:1, one launch (start us, length us, event | category | flops | bytes accessed | tf_op | source)
XLA Modules:
  0.0 82.5 jit_solution(15894802515004781235)
XLA Ops:
  0.6 0.0 copy-start
  0.6 0.0 copy-start.1
  0.7 1.3 %copy.15.state_weight = bf16[2048,32]{1,0:T(8,128)(2,1)S(1)} copy(bf16[2048,32]{0,1:T(8,128)(2,1)} %param.17) | data formatting | bytes 262144 | tf_op args[6]
  1.9 0.0 copy-start.2
  1.9 0.0 copy-start.3
  1.9 0.0 copy-start.4
  2.0 0.0 copy-start.5
  2.0 0.0 copy-start.6
  2.0 1.0 %copy.16.step_weight = bf16[2048,8]{1,0:T(8,128)(2,1)S(1)} copy(bf16[2048,8]{0,1:T(8,128)(2,1)} %param.18) | data formatting | bytes 65536 | tf_op args[7]
  3.0 0.0 copy-done
  3.0 0.0 copy-done.1
  3.1 0.0 copy-done.2
  3.1 0.0 copy-done.3
  3.1 0.0 copy-done.4
  3.1 0.0 copy-done.5
  3.1 0.0 copy-done.6
  3.1 0.0 copy-start.8
  3.1 75.6 %whole_step.1 = (f32[16,256]{1,0:T(8,128)S(1)}, f32[1,128]{1,0:T(1,128)S(1)}) custom-call(bf16[128,2048]{1,0:T(8,128)(2,1)S(1)} %copy-done, bf16[128,2048]{1,0:T(8,128)(2,1)S(1)} %copy-done.1, f32[16,256]{1,0:T(8,128)S(1)} %copy-done.2, bf16[16,1024]{1,0:T(8,128)(2,1)S(1)} %copy-done.3, bf16[2048,32]{1,0:T(8,128)(2,1)S(1)} %copy.15.state_weight, ...), custom_call_target="tpu_custom_call" | custom-call | tf_op jit(solution)/shard_map/whole_step/pallas_call | solution.py:426
  78.7 0.0 copy-start.7
  78.7 0.6 fusion.2
  80.7 0.0 copy-done.8
  80.7 0.0 copy-done.7
  80.7 0.6 multiply_add_fusion
Async XLA Ops:
  0.6 2.4 %copy-start = (bf16[128,2048]{1,0:T(8,128)(2,1)S(1)}, bf16[128,2048]{1,0:T(8,128)(2,1)}, u32[]{:S(2)}) copy-start(bf16[128,2048]{1,0:T(8,128)(2,1)} %tokens.1) | copy-start | bytes 1572868
  0.6 2.4 %copy-start.1 = (bf16[128,2048]{1,0:T(8,128)(2,1)S(1)}, bf16[128,2048]{1,0:T(8,128)(2,1)}, u32[]{:S(2)}) copy-start(bf16[128,2048]{1,0:T(8,128)(2,1)} %teacher.1) | copy-start | bytes 1572868
  1.9 1.1 %copy-start.2 = (f32[16,256]{1,0:T(8,128)S(1)}, f32[16,256]{1,0:T(8,128)}, u32[]{:S(2)}) copy-start(f32[16,256]{1,0:T(8,128)} %inner_weight.1) | copy-start | bytes 49156
  1.9 1.1 %copy-start.3 = (bf16[16,1024]{1,0:T(8,128)(2,1)S(1)}, bf16[16,1024]{1,0:T(8,128)(2,1)}, u32[]{:S(2)}) copy-start(bf16[16,1024]{1,0:T(8,128)(2,1)} %output_weight.1) | copy-start | bytes 98308
  1.9 1.1 %copy-start.4 = (f32[8]{0:T(128)S(1)}, f32[8]{0:T(128)}, u32[]{:S(2)}) copy-start(f32[8]{0:T(128)} %param.19) | copy-start | bytes 100
  2.0 1.1 %copy-start.5 = (f32[8]{0:T(128)S(1)}, f32[8]{0:T(128)}, u32[]{:S(2)}) copy-start(f32[8]{0:T(128)} %param.20) | copy-start | bytes 100
  2.0 1.1 %copy-start.6 = (f32[8]{0:T(128)S(1)}, f32[8]{0:T(128)}, u32[]{:S(2)}) copy-start(f32[8]{0:T(128)} %param.21) | copy-start | bytes 100
  3.1 77.6 %copy-start.8 = (f32[16,256]{1,0:T(8,128)S(1)}, f32[16,256]{1,0:T(8,128)}, u32[]{:S(2)}) copy-start(f32[16,256]{1,0:T(8,128)} %param.16) | copy-start | bytes 49156
  78.7 2.0 %copy-start.7 = (f32[16,256]{1,0:T(8,128)S(1)}, f32[16,256]{1,0:T(8,128)}, u32[]{:S(2)}) copy-start(f32[16,256]{1,0:T(8,128)} %param.15) | copy-start | bytes 49156

commit v4 on v3

--- a/solution.py
+++ b/solution.py
@@ -22,8 +22,8 @@
 
 
 TORUS = ("dp_0", "dp_1", "dp_2")
-BY_COLUMN = ("dp_2", "dp_1", "dp_0")
-BY_ROW = ("dp_2", "dp_0", "dp_1")
+BY_COLUMN = (("dp_2", "dp_1", "dp_0"), 2)
+BY_ROW = (("dp_0", "dp_2", "dp_1"), 1)
 CHUNK = 256
 
 
@@ -51,14 +51,18 @@
                 out.append(nxt)
         return out
 
-    def children(rel, order):
+    def children(rel, tree):
+        order, straight = tree
         out = onward(rel, order)
+        zero = {a: 0 for a in TORUS}
         if not any(rel.values()):
             for i in range(sizes[order[0]]):
-                for j in range(sizes[order[1]]):
+                for j in range(sizes[order[1]] if straight == 2 else 1):
                     if i or j:
-                        out.append({order[0]: i, order[1]: j, order[2]: 0})
-            out.sort(key=lambda r: -sum(min(v, sizes[a] - v) for a, v in r.items()))
+                        out.append({**zero, order[0]: i, order[1]: j})
+        if straight == 1 and rel[order[1]] == 0 and rel[order[2]] == 0:
+            out += [{**rel, order[1]: j} for j in range(1, sizes[order[1]])]
+        out.sort(key=lambda r: -sum(min(v, sizes[a] - v) for a, v in r.items()))
         return out
 
     return children
@@ -93,8 +97,12 @@
 
 
 def step_kernel(
-    sizes, tokens, teacher, inner_weight, output_weight, state_weight, step_weight,
-    step_bias, decay_log, skip, grad_out, sums_out,
+    sizes,
+    tokens_hbm, teacher_hbm, inner_weight_hbm, output_weight_hbm, state_weight_hbm,
+    step_weight_hbm, step_bias_hbm, decay_log_hbm, skip_hbm,
+    loss_out, clipped_out,
+    tokens, teacher, inner_weight, output_weight, state_weight,
+    step_weight, step_bias, decay_log, skip, load_sem,
     mine, in_all, w_all, mix, mix_t, inner,
     tok_t, tok_all, part, leaving, arrived, grad_acc, gp_all, g_part, g_all, row_a, row_b,
     in_send, in_recv, in_pair, w_send, w_recv, w_pair,
@@ -129,13 +137,26 @@
         for i in range(nx) for j in range(ny) for k in range(2) for t in range(2)
     ][1:]
     column = [dict(dp_0=i, dp_2=j) for i in range(nz) for j in range(ny)][1:]
-    peers = plane + [by for by in column if by["dp_0"]]
+    peers = plane + [dict(dp_0=i) for i in range(1, nz)]
     pair = there(dp_3=1)
+    loads = [
+        pltpu.make_async_copy(source, target, load_sem.at[n])
+        for n, (source, target) in enumerate((
+            (inner_weight_hbm, inner_weight), (output_weight_hbm, output_weight),
+            (tokens_hbm, tokens), (state_weight_hbm, state_weight),
+            (step_weight_hbm, step_weight), (step_bias_hbm, step_bias),
+            (decay_log_hbm, decay_log), (skip_hbm, skip), (teacher_hbm, teacher),
+        ))
+    ]
+    for load in loads:
+        load.start()
     barrier = pltpu.get_barrier_semaphore()
     for by in peers:
         pl.semaphore_signal(
             barrier, inc=1, device_id=there(**by), device_id_type=pl.DeviceIdType.MESH
         )
+    for load in loads[:2]:
+        load.wait()
     mine[...] = inner_weight[...].astype(jnp.bfloat16)
     in_all[here["dp_0"], here["dp_1"], here["dp_2"], core] = mine[...]
     w_all[here["dp_0"], here["dp_1"], here["dp_2"], core] = output_weight[...]
@@ -143,7 +164,7 @@
     in_wire, w_wire = 0.088, 0.352
     flows = (
         (BY_ROW, in_wire, 0.0), (BY_ROW, in_wire, 0.0),
-        (BY_COLUMN, w_wire, 0.01), (BY_ROW, w_wire, 0.01),
+        (BY_COLUMN, w_wire, 0.01), (BY_COLUMN, w_wire, 0.01),
     )
     events = relay_times(sizes, flows)
     steps = [
@@ -192,7 +213,10 @@
             tok_t[z, x : x + 128 // rows_x] = turned.reshape(128 // rows_x, ny, 2, per, seq)
 
     def mix_heads():
-        projected = jnp.dot(tokens[...], state_weight[...], preferred_element_type=jnp.float32)
+        projected = lax.dot_general(
+            tokens[...], state_weight[...], (((1,), (1,)), ((), ())),
+            preferred_element_type=jnp.float32,
+        )
         width = projected.shape[1] // 2
         b_coef, c_coef = projected[:, :width], projected[:, width:]
         gram = lax.dot_general(
@@ -200,7 +224,10 @@
             precision=lax.Precision.HIGHEST, preferred_element_type=jnp.float32,
         )
         raw = (
-            jnp.dot(tokens[...], step_weight[...], preferred_element_type=jnp.float32)
+            lax.dot_general(
+                tokens[...], step_weight[...], (((1,), (1,)), ((), ())),
+                preferred_element_type=jnp.float32,
+            )
             + step_bias[...]
         )
         step_size = jnp.maximum(raw, 0.0) + jnp.log1p(jnp.exp(-jnp.abs(raw)))
@@ -271,6 +298,8 @@
     late = max(t for t, *_ in steps[0] + steps[1]) + 1
     inner_done = max(t for c in range(2) for t, kind, *_ in steps[c] if kind == 0) + 1e-6
     relay_until(0, 2.0)
+    for load in loads[2:]:
+        load.wait()
     turn_tokens()
     relay_until(2.0, 6.0)
     mix_heads()
@@ -280,19 +309,6 @@
     beside = in_all.at[:, :, :, 0]
     remote(beside, beside, in_send, in_pair, pair).wait_recv()
     project()
-    reached = max(inner_done, 9.0)
-    for i in range(chunks):
-        needed = max(
-            t for c in range(2) for t, kind, rel, _ in steps[c]
-            if kind == 1 and rel["dp_0"] == order[i]
-        ) + 1e-6
-        if needed > reached:
-            relay_until(reached, needed)
-            reached = needed
-        student(i)
-    relay_until(reached, late)
-    student_copy(chunks - 1).start()
-
     tok_sends = []
     for i in range(nx):
         for k in range(2):
@@ -307,6 +323,19 @@
         ).start()
     tok_all[0] = tok_t[:, here["dp_1"], :, here["dp_3"]]
 
+    reached = max(inner_done, 9.0)
+    for i in range(chunks):
+        needed = max(
+            t for c in range(2) for t, kind, rel, _ in steps[c]
+            if kind == 1 and rel["dp_0"] == order[i]
+        ) + 1e-6
+        if needed > reached:
+            relay_until(reached, needed)
+            reached = needed
+        student(i)
+    relay_until(reached, late)
+    student_copy(chunks - 1).start()
+
     squares = jnp.zeros((8, CHUNK), jnp.float32)
     for i in range(chunks):
         student_copy(i).wait_recv()
@@ -322,63 +351,65 @@
             grad_acc[...] = product
         else:
             grad_acc[...] += product
+    near = (1, 3, 2) if nx == 4 else range(1, nx)
+    members = 2 * nx
+
+    def gp_copy(g, source, slot, target):
+        return remote(
+            gp_all.at[g, source], gp_all.at[g, slot], gp_send, gp_recv.at[g, slot], target
+        )
+
     for g in range(groups):
-        heads = []
+        heads_here = []
         direct = None
         for h in range(per_group):
-            at = slice((g * per_group + h) * head_dim, (g * per_group + h + 1) * head_dim)
-            one = grad_acc[:, at].astype(jnp.bfloat16)
-            heads.append(one)
             n = g * per_group + h
+            one = grad_acc[:, n * head_dim : (n + 1) * head_dim].astype(jnp.bfloat16)
+            heads_here.append(one)
             term = skip[:, n : n + 1] * one.astype(jnp.float32)
             direct = term if direct is None else direct + term
         back = jnp.dot(
-            mix_t[g], jnp.concatenate(heads, axis=0), preferred_element_type=jnp.float32
-        )
-        gp_all[0, :, g * head_dim : (g + 1) * head_dim] = (back + direct).astype(jnp.bfloat16)
-
-    for i in (2, 1, 3) if nx == 4 else range(1, nx):
-        remote(
-            gp_all.at[0], gp_all.at[2 * i], gp_send, gp_recv.at[2 * i], there(dp_1=i)
-        ).start()
-    remote(gp_all.at[0], gp_all.at[1], gp_send, gp_recv.at[1], pair).start()
-    members = 2 * nx
+            mix_t[g], jnp.concatenate(heads_here, axis=0), preferred_element_type=jnp.float32
+        )
+        gp_all[g, 0] = (back + direct).astype(jnp.bfloat16)
+        for i in reversed(near):
+            gp_copy(g, 0, 2 * i, there(dp_1=i)).start()
+        gp_copy(g, 0, 1, pair).start()
     remote(
         tok_all.at[pl.ds(1, members - 1)], tok_all.at[pl.ds(1, members - 1)],
         tok_send, tok_recv, pair,
     ).wait()
 
-    def product_of(slot):
+    def product_of(g, slot):
         left = tok_all[slot].reshape(-1, seq)
-        return jnp.dot(left, gp_all[slot], preferred_element_type=jnp.float32)
-
-    remote(gp_all.at[1], gp_all.at[1], gp_send, gp_recv.at[1], pair).wait_recv()
-    total = product_of(0) + product_of(1)
-    near = (1, 3, 2) if nx == 4 else range(1, nx)
-    for i in near:
-        remote(gp_all.at[0], gp_all.at[2 * i], gp_send, gp_recv.at[2 * i], pair).wait_recv()
-        remote(
-            gp_all.at[2 * i], gp_all.at[2 * i + 1], gp_send, gp_recv.at[2 * i + 1], pair
-        ).start()
-        total = total + product_of(2 * i)
-    for i in near:
-        remote(
-            gp_all.at[0], gp_all.at[2 * i + 1], gp_send, gp_recv.at[2 * i + 1], pair
-        ).wait_recv()
-        total = total + product_of(2 * i + 1)
-    g_part[...] = total.reshape(g_part.shape)
-
-    for by in sorted(column, key=lambda b: -min(b["dp_0"], nz - b["dp_0"]) - b["dp_2"]):
-        slot = by["dp_0"] * ny + by["dp_2"]
-        to_z = lax.rem(here["dp_0"] + by["dp_0"], nz)
-        to_y = lax.rem(here["dp_2"] + by["dp_2"], ny)
-        remote(g_part.at[to_z, to_y], g_all.at[slot], g_send, g_recv, there(**by)).start()
-    g_all[0] = g_part[here["dp_0"], here["dp_2"]]
+        return jnp.dot(left, gp_all[g, slot], preferred_element_type=jnp.float32)
+
+    outward = sorted(column, key=lambda b: -min(b["dp_0"], nz - b["dp_0"]) - b["dp_2"])
+    for g in range(groups):
+        gp_copy(g, 1, 1, pair).wait_recv()
+        total = product_of(g, 0) + product_of(g, 1)
+        for i in near:
+            gp_copy(g, 0, 2 * i, pair).wait_recv()
+            gp_copy(g, 2 * i, 2 * i + 1, pair).start()
+            total = total + product_of(g, 2 * i)
+        for i in near:
+            gp_copy(g, 0, 2 * i + 1, pair).wait_recv()
+            total = total + product_of(g, 2 * i + 1)
+        g_part[g] = total.reshape(g_part.shape[1:])
+        for by in outward:
+            slot = by["dp_0"] * ny + by["dp_2"]
+            to_z, to_y = ahead("dp_0", by["dp_0"]), ahead("dp_2", by["dp_2"])
+            remote(
+                g_part.at[g, to_z, to_y], g_all.at[g, slot], g_send, g_recv.at[g], there(**by)
+            ).start()
+        g_all[g, 0] = g_part[g, here["dp_0"], here["dp_2"]]
     err = jnp.sum(squares) * 0.5
-    rest = g_all.at[pl.ds(1, nz * ny - 1)]
-    remote(rest, rest, g_send, g_recv, pair).wait()
-    grad = jnp.sum(g_all[...], axis=0)
-    grad_out[...] = grad
+    halves = []
+    for g in range(groups):
+        rest = g_all.at[g, pl.ds(1, nz * ny - 1)]
+        remote(rest, rest, g_send, g_recv.at[g], pair).wait_recv()
+        halves.append(jnp.sum(g_all[g], axis=0))
+    grad = jnp.concatenate(halves, axis=1)
     lane = lax.broadcasted_iota(jnp.int32, (1, 128), 1)
     row = jnp.where(lane == 0, jnp.sum(grad * grad), jnp.where(lane == 1, err, 0.0))
     row_a[0] = row
@@ -391,10 +422,16 @@
         remote(row_b.at[0], row_b.at[i], b_send, b_recv, there(dp_0=i)).start()
     rest = row_b.at[pl.ds(1, nz - 1)]
     remote(rest, rest, b_send, b_recv, pair).wait()
-    sums_out[...] = jnp.sum(row_b[...], axis=0)
-
-    rest = gp_all.at[pl.ds(1, members - 1)]
-    remote(rest, rest, gp_send, gp_recv.at[1], pair).wait_send()
+    sums = jnp.sum(row_b[...], axis=0)
+    root_mean = jnp.sqrt(sums[:, 0:1] / (features * inner_weight.shape[1] * 2))
+    factor = jnp.minimum(1.0, 1.0 / (root_mean + norm_eps))
+    loss_out[...] = jnp.broadcast_to(sums[:, 1:2] / (nz * nx * ny * 2 * seq * features), (1, 128))
+    clipped_out[...] = factor * grad
+    for g in range(groups):
+        rest = gp_all.at[g, pl.ds(1, members - 1)]
+        remote(rest, rest, gp_send, gp_recv.at[g, 1], pair).wait_send()
+        rest = g_all.at[g, pl.ds(1, nz * ny - 1)]
+        remote(rest, rest, g_send, g_recv.at[g], pair).wait_send()
     remote(leaving, leaving, student_send, student_recv.at[0], pair).wait_send()
     pieces = nz * nx * ny
     for block, ref, send in (((0,), in_all, in_send), ((0,), w_all, w_send)):
@@ -427,12 +464,22 @@
         functools.partial(step_kernel, sizes),
         name="whole_step",
         out_shape=(
+            jax.ShapeDtypeStruct((1, 128), f32),
             jax.ShapeDtypeStruct((own_rows, gcols), f32),
-            jax.ShapeDtypeStruct((1, 128), f32),
         ),
-        in_specs=[vmem] * 9,
-        out_specs=(vmem, vmem),
+        in_specs=[pl.BlockSpec(memory_space=pl.ANY)] * 9,
+        out_specs=(vmem,) * 2,
         scratch_shapes=[
+            pltpu.VMEM((seq, features), half),
+            pltpu.VMEM((seq, features), half),
+            pltpu.VMEM((own_rows, gcols), f32),
+            pltpu.VMEM((own_rows, cols), half),
+            pltpu.VMEM((state_weight.shape[1], features), half),
+            pltpu.VMEM((heads, features), half),
+            pltpu.VMEM((1, heads), f32),
+            pltpu.VMEM((1, heads), f32),
+            pltpu.VMEM((1, heads), f32),
+            dma((9,)),
             pltpu.VMEM((own_rows, gcols), half),
             pltpu.VMEM((nz, nx, ny, 2, own_rows, gcols), half),
             pltpu.VMEM((nz, nx, ny, 2, own_rows, cols), half),
@@ -445,20 +492,20 @@
             pltpu.VMEM((chunks, seq, CHUNK), half),
             pltpu.VMEM((chunks, seq, CHUNK), half),
             pltpu.VMEM((seq, cols), f32),
-            pltpu.VMEM((2 * nx, seq, gcols), half),
-            pltpu.VMEM((nz, ny, own_rows, gcols), f32),
-            pltpu.VMEM((nz * ny, own_rows, gcols), f32),
+            pltpu.VMEM((groups, 2 * nx, seq, HEAD_DIM), half),
+            pltpu.VMEM((groups, nz, ny, own_rows, HEAD_DIM), f32),
+            pltpu.VMEM((groups, nz * ny, own_rows, HEAD_DIM), f32),
             pltpu.VMEM((nx * ny * 4, 1, 128), f32),
             pltpu.VMEM((nz, 1, 128), f32),
             dma, dma((nz * nx * ny,)), dma, dma, dma((nz * nx * ny,)), dma((nz,)),
-            dma, dma((chunks,)), dma, dma, dma, dma((2 * nx,)),
-            dma, dma, dma, dma, dma, dma,
+            dma, dma((chunks,)), dma, dma, dma, dma((groups, 2 * nx)),
+            dma, dma((groups,)), dma, dma, dma, dma,
         ],
         compiler_params=pltpu.CompilerParams(
-            collective_id=0, has_side_effects=True, vmem_limit_bytes=40 * 1024 * 1024
+            collective_id=0, has_side_effects=True, vmem_limit_bytes=60 * 1024 * 1024
         ),
     )(
-        tokens, teacher, inner_weight, output_weight, state_weight, step_weight,
+        tokens, teacher, inner_weight, output_weight, state_weight.T, step_weight.T,
         step_bias[None, :], decay_log[None, :], skip_gain[None, :],
     )
 
@@ -476,28 +523,19 @@
     decay_log,
     skip_gain,
 ):
-    seq_rows, model_width = tokens.shape
-    groups_here = inner_weight.shape[1] // HEAD_DIM
-    total_tokens = seq_rows * lax.axis_size(DP)
-    inner_grad, sums = whole_step(
+    loss, clipped = whole_step(
         tokens, teacher, inner_weight, output_weight, state_weight, step_weight,
         step_bias, decay_log, skip_gain,
     )
-    squares_total, error_total = sums[0, 0], sums[0, 1]
-    entry_count = model_width * groups_here * HEAD_DIM * lax.axis_size("tensor")
-    root_mean = jnp.sqrt(squares_total / entry_count)
-    factor = jnp.minimum(1.0, 1.0 / (root_mean + norm_eps))
-    distill_loss = error_total / (total_tokens * model_width)
     first_fix = 1.0 - beta_one**STEP
     second_fix = 1.0 - beta_two**STEP
-    clipped = factor * inner_grad
     first_next = beta_one * inner_first + (1.0 - beta_one) * clipped
     second_next = beta_two * inner_second + (1.0 - beta_two) * clipped * clipped
     update = (
         first_next / first_fix / (jnp.sqrt(second_next / second_fix) + adam_eps)
         + weight_decay * inner_weight
     )
-    return (distill_loss, update, first_next, second_next)
+    return (loss[0, 0], update, first_next, second_next)
 
 
 def solution(mesh):

time: 82.7 us -> 76.1 us (0.920)
  Pallas kernels: 75.6 us -> 72 us
  local copies, waits for them, and re-layouts: 2.95 us -> 0.69 us
  between operations: 3.31 us -> 1.86 us
    pallas_call x1, Pallas kernels: 75.6 us -> 72 us  [whole_step(): pl.pallas_call(functools.partial(step_kernel, sizes), name='whole_step',...]
    unnamed x20 -> x8, local copies, waits for them, and re-layouts: 2.36 us -> 0.69 us
where the time goes in v4:
time: 76.1 us; the launch traced here: 75.9 us
  Pallas kernels  72 us (95%)
  between operations  1.86 us (2%)
  other arithmetic  1.35 us (2%)
    pallas_call x1, Pallas kernels, whole_step(): pl.pallas_call(functools.partial(step_kernel, sizes), name='whole_step',...  72 us

profile of v4, /device:TPU:1, one launch (start us, length us, event | category | flops | bytes accessed | tf_op | source)
XLA Modules:
  0.0 75.9 jit_solution(14864542786212072290)
XLA Ops:
  0.6 0.0 copy-start
  0.6 0.0 copy-start.1
  0.7 0.0 copy-start.2
  0.7 72.0 %whole_step.1 = (f32[1,128]{1,0:T(1,128)}, f32[16,256]{1,0:T(8,128)}) custom-call(bf16[128,2048]{1,0:T(8,128)(2,1)} %tokens_hbm.1, bf16[128,2048]{1,0:T(8,128)(2,1)} %teacher_hbm.1, f32[16,256]{1,0:T(8,128)} %inner_weight_hbm.1, bf16[16,1024]{1,0:T(8,128)(2,1)} %output_weight_hbm.1, bf16[32,2048]{1,0:T(8,128)(2,1)} %bitcast.7, bf16[8,2048]{1,0:T(8,128)(2,1)} %bitcast.8, ...), custom_call_target="tpu_custom_call" | custom-call | tf_op jit(solution)/shard_map/whole_step/pallas_call | solution.py:463
  72.6 0.0 copy-done
  72.6 0.0 copy-done.1
  72.7 0.0 copy-done.2
  72.7 1.3 %multiply_add_fusion = (f32[16,256]{1,0:T(8,128)}, f32[16,256]{1,0:T(8,128)}, f32[16,256]{1,0:T(8,128)}) fusion(f32[16,256]{1,0:T(8,128)S(1)} %copy-done, f32[16,256]{1,0:T(8,128)} %get-tuple-element.7, f32[16,256]{1,0:T(8,128)S(1)} %copy-done.1, f32[16,256]{1,0:T(8,128)S(1)} %copy-done.2), kind=kLoop, calls=%fused_computation.2 | loop fusion | flops 53248 | bytes 114688 | tf_op jit(solution)/shard_map/add | solution.py:535
  74.0 0.0 copy-start.3
  74.0 0.7 copy-done.3
Async XLA Ops:
  0.6 72.0 %copy-start = (f32[16,256]{1,0:T(8,128)S(1)}, f32[16,256]{1,0:T(8,128)}, u32[]{:S(2)}) copy-start(f32[16,256]{1,0:T(8,128)} %inner_weight_hbm.1) | copy-start | bytes 49156
  0.6 72.0 %copy-start.1 = (f32[16,256]{1,0:T(8,128)S(1)}, f32[16,256]{1,0:T(8,128)}, u32[]{:S(2)}) copy-start(f32[16,256]{1,0:T(8,128)} %param.15) | copy-start | bytes 49156
  0.7 72.0 %copy-start.2 = (f32[16,256]{1,0:T(8,128)S(1)}, f32[16,256]{1,0:T(8,128)}, u32[]{:S(2)}) copy-start(f32[16,256]{1,0:T(8,128)} %param.16) | copy-start | bytes 49156
  74.0 0.7 copy-start.3

commit v5 on v4

--- a/solution.py
+++ b/solution.py
@@ -22,9 +22,11 @@
 
 
 TORUS = ("dp_0", "dp_1", "dp_2")
-BY_COLUMN = (("dp_2", "dp_1", "dp_0"), 2)
-BY_ROW = (("dp_0", "dp_2", "dp_1"), 1)
+BY_COLUMN = (("dp_2", "dp_1", "dp_0"), 2, False)
+BY_ROW = (("dp_0", "dp_2", "dp_1"), 1, True)
 CHUNK = 256
+NARROW = 2
+MIX_AT = 9.0
 
 
 def ways(sizes):
@@ -52,8 +54,12 @@
         return out
 
     def children(rel, tree):
-        order, straight = tree
-        out = onward(rel, order)
+        order, straight, jump = tree
+        last = order[2]
+        if jump:
+            out = [{**rel, last: v} for v in range(1, sizes[last])] if rel[last] == 0 else []
+        else:
+            out = onward(rel, order)
         zero = {a: 0 for a in TORUS}
         if not any(rel.values()):
             for i in range(sizes[order[0]]):
@@ -91,7 +97,7 @@
                     free[(a, go)] = begin + wire * far
                     lands = max(lands, begin + wire)
                     hops += far
-            heapq.heappush(heap, (lands + latency + hop * (hops - 1), count, n, nxt))
+            heapq.heappush(heap, (lands + latency + hop * (hops - 1) + (0.8 if n % 2 == 0 else 0.0), count, n, nxt))
             count += 1
     return events
 
@@ -102,9 +108,9 @@
     step_weight_hbm, step_bias_hbm, decay_log_hbm, skip_hbm,
     loss_out, clipped_out,
     tokens, teacher, inner_weight, output_weight, state_weight,
-    step_weight, step_bias, decay_log, skip, load_sem,
+    step_weight, step_bias, decay_log, skip, load_sem, lend_send, lend_recv,
     mine, in_all, w_all, mix, mix_t, inner,
-    tok_t, tok_all, part, leaving, arrived, grad_acc, gp_all, g_part, g_all, row_a, row_b,
+    tok_t, tok_all, part, leaving, arrived, arrived_wide, grad_acc, gp_all, g_part, g_half, g_all, row_a, row_b,
     in_send, in_recv, in_pair, w_send, w_recv, w_pair,
     student_send, student_recv, tok_send, tok_recv, gp_send, gp_recv,
     g_send, g_recv, a_send, a_recv, b_send, b_recv,
@@ -143,13 +149,25 @@
         pltpu.make_async_copy(source, target, load_sem.at[n])
         for n, (source, target) in enumerate((
             (inner_weight_hbm, inner_weight), (output_weight_hbm, output_weight),
-            (tokens_hbm, tokens), (state_weight_hbm, state_weight),
-            (step_weight_hbm, step_weight), (step_bias_hbm, step_bias),
-            (decay_log_hbm, decay_log), (skip_hbm, skip), (teacher_hbm, teacher),
+            (state_weight_hbm, state_weight), (step_weight_hbm, step_weight),
+            (step_bias_hbm, step_bias), (decay_log_hbm, decay_log), (skip_hbm, skip),
+            (tokens_hbm, tokens), (teacher_hbm, teacher),
         ))
     ]
-    for load in loads:
+    borrows = jnp.logical_and(core == 1, here["tensor"] == 1)
+    lends = jnp.logical_and(core == 1, here["tensor"] == 0)
+    lent = [
+        remote(ref, ref, lend_send.at[n], lend_recv.at[n], there(tensor=1, dp_2=1))
+        for n, ref in enumerate((tokens, teacher))
+    ]
+    for load in loads[:-2]:
         load.start()
+
+    @pl.when(jnp.logical_not(borrows))
+    def _():
+        for load in loads[-2:]:
+            load.start()
+
     barrier = pltpu.get_barrier_semaphore()
     for by in peers:
         pl.semaphore_signal(
@@ -269,13 +287,21 @@
                     mixed[h * seq : (h + 1) * seq] + skip[:, n : n + 1] * wide
                 ).astype(jnp.bfloat16)
 
-    other_half = there(tensor=1)
+    other_half = {"tensor": 1 - here["tensor"], "dp_2": lax.rem(here["dp_2"] + core, ny)}
     order = sorted(range(nz), key=lambda v: (min(v, nz - v), v))
 
+    wide = chunks - leaving.shape[0]
+
     def student_copy(i):
+        source, target = (part, arrived_wide) if i < wide else (leaving, arrived)
+        at = i if i < wide else i - wide
         return remote(
-            leaving.at[i], arrived.at[i], student_send, student_recv.at[i], other_half
-        )
+            source.at[at], target.at[at], student_send.at[int(i < wide)],
+            student_recv.at[i], other_half,
+        )
+
+    def came(i):
+        return arrived_wide[i] if i < wide else arrived[i - wide].astype(jnp.float32)
 
     def w_rows(i):
         return w_all[ahead("dp_0", -order[i])].reshape(CHUNK, cols)
@@ -290,22 +316,37 @@
             inner[...], w_rows(i), (((1,), (1,)), ((), ())), preferred_element_type=jnp.float32
         )
         part[i] = piece
-        leaving[i] = piece.astype(jnp.bfloat16)
+        if i >= wide:
+            leaving[i - wide] = piece.astype(jnp.bfloat16)
         if i:
             student_copy(i - 1).start()
 
     pl.semaphore_wait(barrier, len(peers))
     late = max(t for t, *_ in steps[0] + steps[1]) + 1
     inner_done = max(t for c in range(2) for t, kind, *_ in steps[c] if kind == 0) + 1e-6
+    @pl.when(jnp.logical_not(borrows))
+    def _():
+        for load in loads[-2:]:
+            load.wait()
+
+    @pl.when(lends)
+    def _():
+        for copy in lent:
+            copy.start()
+
     relay_until(0, 2.0)
-    for load in loads[2:]:
+    for load in loads[2:-2]:
         load.wait()
+    relay_until(2.0, MIX_AT)
+
+    @pl.when(borrows)
+    def _():
+        lent[0].wait_recv()
+
     turn_tokens()
-    relay_until(2.0, 6.0)
     mix_heads()
-    relay_until(6.0, 9.0)
     turn_mix()
-    relay_until(9.0, max(inner_done, 9.0))
+    relay_until(MIX_AT, max(inner_done, MIX_AT))
     beside = in_all.at[:, :, :, 0]
     remote(beside, beside, in_send, in_pair, pair).wait_recv()
     project()
@@ -323,7 +364,7 @@
         ).start()
     tok_all[0] = tok_t[:, here["dp_1"], :, here["dp_3"]]
 
-    reached = max(inner_done, 9.0)
+    reached = max(inner_done, MIX_AT)
     for i in range(chunks):
         needed = max(
             t for c in range(2) for t, kind, rel, _ in steps[c]
@@ -336,11 +377,20 @@
     relay_until(reached, late)
     student_copy(chunks - 1).start()
 
+    @pl.when(borrows)
+    def _():
+        lent[1].wait_recv()
+
+    @pl.when(lends)
+    def _():
+        for copy in lent:
+            copy.wait_send()
+
     squares = jnp.zeros((8, CHUNK), jnp.float32)
     for i in range(chunks):
         student_copy(i).wait_recv()
         error = (
-            part[i] + arrived[i].astype(jnp.float32)
+            part[i] + came(i)
             - teacher_cols(i).astype(jnp.float32)
         )
         squares = squares + jnp.sum((error * error).reshape(seq // 8, 8, CHUNK), axis=0)
@@ -395,20 +445,23 @@
         for i in near:
             gp_copy(g, 0, 2 * i + 1, pair).wait_recv()
             total = total + product_of(g, 2 * i + 1)
+        g_half[g] = total.reshape(g_part.shape[1:]).astype(jnp.bfloat16)
         g_part[g] = total.reshape(g_part.shape[1:])
         for by in outward:
             slot = by["dp_0"] * ny + by["dp_2"]
             to_z, to_y = ahead("dp_0", by["dp_0"]), ahead("dp_2", by["dp_2"])
             remote(
-                g_part.at[g, to_z, to_y], g_all.at[g, slot], g_send, g_recv.at[g], there(**by)
+                g_half.at[g, to_z, to_y], g_all.at[g, slot], g_send, g_recv.at[g], there(**by)
             ).start()
-        g_all[g, 0] = g_part[g, here["dp_0"], here["dp_2"]]
     err = jnp.sum(squares) * 0.5
     halves = []
     for g in range(groups):
         rest = g_all.at[g, pl.ds(1, nz * ny - 1)]
         remote(rest, rest, g_send, g_recv.at[g], pair).wait_recv()
-        halves.append(jnp.sum(g_all[g], axis=0))
+        halves.append(
+            g_part[g, here["dp_0"], here["dp_2"]]
+            + jnp.sum(g_all[g, 1:].astype(jnp.float32), axis=0)
+        )
     grad = jnp.concatenate(halves, axis=1)
     lane = lax.broadcasted_iota(jnp.int32, (1, 128), 1)
     row = jnp.where(lane == 0, jnp.sum(grad * grad), jnp.where(lane == 1, err, 0.0))
@@ -432,7 +485,8 @@
         remote(rest, rest, gp_send, gp_recv.at[g, 1], pair).wait_send()
         rest = g_all.at[g, pl.ds(1, nz * ny - 1)]
         remote(rest, rest, g_send, g_recv.at[g], pair).wait_send()
-    remote(leaving, leaving, student_send, student_recv.at[0], pair).wait_send()
+    remote(leaving, leaving, student_send.at[0], student_recv.at[0], pair).wait_send()
+    remote(arrived_wide, arrived_wide, student_send.at[1], student_recv.at[0], pair).wait_send()
     pieces = nz * nx * ny
     for block, ref, send in (((0,), in_all, in_send), ((0,), w_all, w_send)):
         half = ref.at[:, :, :, 0]
@@ -480,6 +534,8 @@
             pltpu.VMEM((1, heads), f32),
             pltpu.VMEM((1, heads), f32),
             dma((9,)),
+            dma((2,)),
+            dma((2,)),
             pltpu.VMEM((own_rows, gcols), half),
             pltpu.VMEM((nz, nx, ny, 2, own_rows, gcols), half),
             pltpu.VMEM((nz, nx, ny, 2, own_rows, cols), half),
@@ -489,16 +545,18 @@
             pltpu.VMEM((nz, nx, ny, 2, own_rows, seq), half),
             pltpu.VMEM((2 * nx, nz, ny, own_rows, seq), half),
             pltpu.VMEM((chunks, seq, CHUNK), f32),
-            pltpu.VMEM((chunks, seq, CHUNK), half),
-            pltpu.VMEM((chunks, seq, CHUNK), half),
+            pltpu.VMEM((NARROW, seq, CHUNK), half),
+            pltpu.VMEM((NARROW, seq, CHUNK), half),
+            pltpu.VMEM((chunks - NARROW, seq, CHUNK), f32),
             pltpu.VMEM((seq, cols), f32),
             pltpu.VMEM((groups, 2 * nx, seq, HEAD_DIM), half),
             pltpu.VMEM((groups, nz, ny, own_rows, HEAD_DIM), f32),
-            pltpu.VMEM((groups, nz * ny, own_rows, HEAD_DIM), f32),
+            pltpu.VMEM((groups, nz, ny, own_rows, HEAD_DIM), half),
+            pltpu.VMEM((groups, nz * ny, own_rows, HEAD_DIM), half),
             pltpu.VMEM((nx * ny * 4, 1, 128), f32),
             pltpu.VMEM((nz, 1, 128), f32),
             dma, dma((nz * nx * ny,)), dma, dma, dma((nz * nx * ny,)), dma((nz,)),
-            dma, dma((chunks,)), dma, dma, dma, dma((groups, 2 * nx)),
+            dma((2,)), dma((chunks,)), dma, dma, dma, dma((groups, 2 * nx)),
             dma, dma((groups,)), dma, dma, dma, dma,
         ],
         compiler_params=pltpu.CompilerParams(

time: 76.1 us -> 72.3 us (0.950)
  Pallas kernels: 72 us -> 68.2 us
    pallas_call x1, Pallas kernels: 72 us -> 68.2 us  [whole_step(): pl.pallas_call(functools.partial(step_kernel, sizes), name='whole_step',...]
where the time goes in v5:
time: 72.3 us; the launch traced here: 72.1 us
  Pallas kernels  68.2 us (94%)
  between operations  1.86 us (3%)
  other arithmetic  1.35 us (2%)
    pallas_call x1, Pallas kernels, whole_step(): pl.pallas_call(functools.partial(step_kernel, sizes), name='whole_step',...  68.2 us

profile of v5, /device:TPU:1, one launch (start us, length us, event | category | flops | bytes accessed | tf_op | source)
XLA Modules:
  0.0 72.1 jit_solution(16227621521478196212)
XLA Ops:
  0.6 0.0 copy-start
  0.6 0.0 copy-start.1
  0.7 0.0 copy-start.2
  0.7 68.2 %whole_step.1 = (f32[1,128]{1,0:T(1,128)}, f32[16,256]{1,0:T(8,128)}) custom-call(bf16[128,2048]{1,0:T(8,128)(2,1)} %tokens_hbm.1, bf16[128,2048]{1,0:T(8,128)(2,1)} %teacher_hbm.1, f32[16,256]{1,0:T(8,128)} %inner_weight_hbm.1, bf16[16,1024]{1,0:T(8,128)(2,1)} %output_weight_hbm.1, bf16[32,2048]{1,0:T(8,128)(2,1)} %bitcast.7, bf16[8,2048]{1,0:T(8,128)(2,1)} %bitcast.8, ...), custom_call_target="tpu_custom_call" | custom-call | tf_op jit(solution)/shard_map/whole_step/pallas_call | solution.py:517
  68.9 0.0 copy-done
  68.9 0.0 copy-done.1
  68.9 0.0 copy-done.2
  68.9 1.3 %multiply_add_fusion = (f32[16,256]{1,0:T(8,128)}, f32[16,256]{1,0:T(8,128)}, f32[16,256]{1,0:T(8,128)}) fusion(f32[16,256]{1,0:T(8,128)S(1)} %copy-done, f32[16,256]{1,0:T(8,128)} %get-tuple-element.7, f32[16,256]{1,0:T(8,128)S(1)} %copy-done.1, f32[16,256]{1,0:T(8,128)S(1)} %copy-done.2), kind=kLoop, calls=%fused_computation.2 | loop fusion | flops 53248 | bytes 114688 | tf_op jit(solution)/shard_map/add | solution.py:593
  70.3 0.0 copy-start.3
  70.3 0.7 copy-done.3
Async XLA Ops:
  0.6 68.2 %copy-start = (f32[16,256]{1,0:T(8,128)S(1)}, f32[16,256]{1,0:T(8,128)}, u32[]{:S(2)}) copy-start(f32[16,256]{1,0:T(8,128)} %inner_weight_hbm.1) | copy-start | bytes 49156
  0.6 68.2 %copy-start.1 = (f32[16,256]{1,0:T(8,128)S(1)}, f32[16,256]{1,0:T(8,128)}, u32[]{:S(2)}) copy-start(f32[16,256]{1,0:T(8,128)} %param.15) | copy-start | bytes 49156
  0.7 68.2 %copy-start.2 = (f32[16,256]{1,0:T(8,128)S(1)}, f32[16,256]{1,0:T(8,128)}, u32[]{:S(2)}) copy-start(f32[16,256]{1,0:T(8,128)} %param.16) | copy-start | bytes 49156
  70.3 0.7 copy-start.3

commit v6 on v5

--- a/solution.py
+++ b/solution.py
@@ -25,7 +25,7 @@
 BY_COLUMN = (("dp_2", "dp_1", "dp_0"), 2, False)
 BY_ROW = (("dp_0", "dp_2", "dp_1"), 1, True)
 CHUNK = 256
-NARROW = 2
+NARROW = 3
 MIX_AT = 9.0
 
 
@@ -74,7 +74,7 @@
     return children
 
 
-def relay_times(sizes, flows, latency=2.45, hop=0.45):
+def relay_times(sizes, flows, latency=2.6, hop=0.45):
     children = ways(sizes)
     free, heap, count = {}, [], 0
     events = [[] for _ in flows]
@@ -97,7 +97,7 @@
                     free[(a, go)] = begin + wire * far
                     lands = max(lands, begin + wire)
                     hops += far
-            heapq.heappush(heap, (lands + latency + hop * (hops - 1) + (0.8 if n % 2 == 0 else 0.0), count, n, nxt))
+            heapq.heappush(heap, (lands + latency + hop * (hops - 1) + (1.0 if n % 2 == 0 else 0.0), count, n, nxt))
             count += 1
     return events
 
@@ -182,7 +182,7 @@
     in_wire, w_wire = 0.088, 0.352
     flows = (
         (BY_ROW, in_wire, 0.0), (BY_ROW, in_wire, 0.0),
-        (BY_COLUMN, w_wire, 0.01), (BY_COLUMN, w_wire, 0.01),
+        (BY_COLUMN, w_wire, -0.01), (BY_COLUMN, w_wire, -0.01),
     )
     events = relay_times(sizes, flows)
     steps = [
@@ -334,7 +334,7 @@
         for copy in lent:
             copy.start()
 
-    relay_until(0, 2.0)
+    relay_until(-1.0, 2.0)
     for load in loads[2:-2]:
         load.wait()
     relay_until(2.0, MIX_AT)

time: 72.3 us -> 70.9 us (0.981)
  Pallas kernels: 68.2 us -> 66.8 us
    pallas_call x1, Pallas kernels: 68.2 us -> 66.8 us  [whole_step(): pl.pallas_call(functools.partial(step_kernel, sizes), name='whole_step',...]
where the time goes in v6:
time: 70.9 us; the launch traced here: 70.7 us
  Pallas kernels  66.8 us (94%)
  between operations  1.86 us (3%)
  other arithmetic  1.35 us (2%)
    pallas_call x1, Pallas kernels, whole_step(): pl.pallas_call(functools.partial(step_kernel, sizes), name='whole_step',...  66.8 us

profile of v6, /device:TPU:1, one launch (start us, length us, event | category | flops | bytes accessed | tf_op | source)
XLA Modules:
  0.0 70.7 jit_solution(15460902086223954751)
XLA Ops:
  0.6 0.0 copy-start
  0.6 0.0 copy-start.1
  0.7 0.0 copy-start.2
  0.7 66.8 %whole_step.1 = (f32[1,128]{1,0:T(1,128)}, f32[16,256]{1,0:T(8,128)}) custom-call(bf16[128,2048]{1,0:T(8,128)(2,1)} %tokens_hbm.1, bf16[128,2048]{1,0:T(8,128)(2,1)} %teacher_hbm.1, f32[16,256]{1,0:T(8,128)} %inner_weight_hbm.1, bf16[16,1024]{1,0:T(8,128)(2,1)} %output_weight_hbm.1, bf16[32,2048]{1,0:T(8,128)(2,1)} %bitcast.7, bf16[8,2048]{1,0:T(8,128)(2,1)} %bitcast.8, ...), custom_call_target="tpu_custom_call" | custom-call | tf_op jit(solution)/shard_map/whole_step/pallas_call | solution.py:517
  67.5 0.0 copy-done
  67.5 0.0 copy-done.1
  67.5 0.0 copy-done.2
  67.5 1.3 %multiply_add_fusion = (f32[16,256]{1,0:T(8,128)}, f32[16,256]{1,0:T(8,128)}, f32[16,256]{1,0:T(8,128)}) fusion(f32[16,256]{1,0:T(8,128)S(1)} %copy-done, f32[16,256]{1,0:T(8,128)} %get-tuple-element.7, f32[16,256]{1,0:T(8,128)S(1)} %copy-done.1, f32[16,256]{1,0:T(8,128)S(1)} %copy-done.2), kind=kLoop, calls=%fused_computation.2 | loop fusion | flops 53248 | bytes 114688 | tf_op jit(solution)/shard_map/add | solution.py:593
  68.9 0.0 copy-start.3
  68.9 0.7 copy-done.3
Async XLA Ops:
  0.6 66.9 %copy-start = (f32[16,256]{1,0:T(8,128)S(1)}, f32[16,256]{1,0:T(8,128)}, u32[]{:S(2)}) copy-start(f32[16,256]{1,0:T(8,128)} %inner_weight_hbm.1) | copy-start | bytes 49156
  0.6 66.9 %copy-start.1 = (f32[16,256]{1,0:T(8,128)S(1)}, f32[16,256]{1,0:T(8,128)}, u32[]{:S(2)}) copy-start(f32[16,256]{1,0:T(8,128)} %param.15) | copy-start | bytes 49156
  0.7 66.9 %copy-start.2 = (f32[16,256]{1,0:T(8,128)S(1)}, f32[16,256]{1,0:T(8,128)}, u32[]{:S(2)}) copy-start(f32[16,256]{1,0:T(8,128)} %param.16) | copy-start | bytes 49156
  68.9 0.7 copy-start.3

commit v7 on v6

--- a/solution.py
+++ b/solution.py
@@ -478,7 +478,7 @@
     sums = jnp.sum(row_b[...], axis=0)
     root_mean = jnp.sqrt(sums[:, 0:1] / (features * inner_weight.shape[1] * 2))
     factor = jnp.minimum(1.0, 1.0 / (root_mean + norm_eps))
-    loss_out[...] = jnp.broadcast_to(sums[:, 1:2] / (nz * nx * ny * 2 * seq * features), (1, 128))
+    loss_out[0, 0] = jnp.sum(jnp.where(lane == 1, sums, 0.0)) / (nz * nx * ny * 2 * seq * features)
     clipped_out[...] = factor * grad
     for g in range(groups):
         rest = gp_all.at[g, pl.ds(1, members - 1)]
@@ -518,11 +518,11 @@
         functools.partial(step_kernel, sizes),
         name="whole_step",
         out_shape=(
-            jax.ShapeDtypeStruct((1, 128), f32),
+            jax.ShapeDtypeStruct((1, 1), f32),
             jax.ShapeDtypeStruct((own_rows, gcols), f32),
         ),
         in_specs=[pl.BlockSpec(memory_space=pl.ANY)] * 9,
-        out_specs=(vmem,) * 2,
+        out_specs=(pl.BlockSpec(memory_space=pltpu.SMEM), vmem),
         scratch_shapes=[
             pltpu.VMEM((seq, features), half),
             pltpu.VMEM((seq, features), half),

time: 70.9 us -> 70.8 us (level)
  no operation moved by 1% of the time
where the time goes in v7:
time: 70.8 us; the launch traced here: 70.6 us
  Pallas kernels  66.9 us (94%)
  between operations  2.38 us (3%)
  other arithmetic  1.35 us (2%)
    pallas_call x1, Pallas kernels, whole_step(): pl.pallas_call(functools.partial(step_kernel, sizes), name='whole_step',...  66.9 us

profile of v7, /device:TPU:1, one launch (start us, length us, event | category | flops | bytes accessed | tf_op | source)
XLA Modules:
  0.0 70.6 jit_solution(15185757649602327861)
XLA Ops:
  0.6 0.0 copy-start
  0.6 0.0 copy-start.1
  0.7 0.0 copy-start.2
  0.7 66.9 %whole_step.1 = (f32[1,1]{1,0:T(1,128)}, f32[16,256]{1,0:T(8,128)}) custom-call(bf16[128,2048]{1,0:T(8,128)(2,1)} %tokens_hbm.1, bf16[128,2048]{1,0:T(8,128)(2,1)} %teacher_hbm.1, f32[16,256]{1,0:T(8,128)} %inner_weight_hbm.1, bf16[16,1024]{1,0:T(8,128)(2,1)} %output_weight_hbm.1, bf16[32,2048]{1,0:T(8,128)(2,1)} %bitcast.6, bf16[8,2048]{1,0:T(8,128)(2,1)} %bitcast.7, ...), custom_call_target="tpu_custom_call" | custom-call | tf_op jit(solution)/shard_map/whole_step/pallas_call | solution.py:517
  67.5 0.0 copy-done
  67.5 0.0 copy-done.1
  67.6 0.0 copy-done.2
  67.6 1.3 %multiply_add_fusion = (f32[16,256]{1,0:T(8,128)}, f32[16,256]{1,0:T(8,128)}, f32[16,256]{1,0:T(8,128)}) fusion(f32[16,256]{1,0:T(8,128)S(1)} %copy-done, f32[16,256]{1,0:T(8,128)} %get-tuple-element.7, f32[16,256]{1,0:T(8,128)S(1)} %copy-done.1, f32[16,256]{1,0:T(8,128)S(1)} %copy-done.2), kind=kLoop, calls=%fused_computation.2 | loop fusion | flops 53248 | bytes 114688 | tf_op jit(solution)/shard_map/add | solution.py:593
Async XLA Ops:
  0.6 66.9 %copy-start = (f32[16,256]{1,0:T(8,128)S(1)}, f32[16,256]{1,0:T(8,128)}, u32[]{:S(2)}) copy-start(f32[16,256]{1,0:T(8,128)} %inner_weight_hbm.1) | copy-start | bytes 49156
  0.6 66.9 %copy-start.1 = (f32[16,256]{1,0:T(8,128)S(1)}, f32[16,256]{1,0:T(8,128)}, u32[]{:S(2)}) copy-start(f32[16,256]{1,0:T(8,128)} %param.15) | copy-start | bytes 49156
  0.7 66.9 %copy-start.2 = (f32[16,256]{1,0:T(8,128)S(1)}, f32[16,256]{1,0:T(8,128)}, u32[]{:S(2)}) copy-start(f32[16,256]{1,0:T(8,128)} %param.16) | copy-start | bytes 49156
